TPU v7x, 32 devices: a whole 2x2x4 slice. The times are simulated.
32 devices in a mesh: dp: 32 (over z, y, x, core), tensor: 1.
Axes of the slice: x: 2, y: 2, z: 4, core: 2. Of those that a mesh axis runs over, the one named last changes fastest.
Arguments:
- master: float32 [3, 4, 1024, 2048], P(None, None, 'dp', 'tensor'), may hold values from -6 to 6
- moment_one: float32 [3, 4, 1024, 2048], P(None, None, 'dp', 'tensor'), may hold values from -4 to 4
- moment_two: float32 [3, 4, 1024, 2048], P(None, None, 'dp', 'tensor'), may hold values from 0.01 to 1
- gradients: bfloat16 [3, 4, 1024, 2048], P(None, None, 'dp', 'tensor'), may hold values from -10000 to 10000
- norm_gain: float32 [2048], replicated, may hold values from 0.1 to 1.9
- hidden_in: bfloat16 [4, 128, 2048], P(None, ('dp', 'tensor')), may hold values from -6 to 6
- expert_ids: int32 [4, 128, 2], P(None, ('dp', 'tensor')), may hold values from 0 to 3, all different within a row; in each aligned block of 4 rows (0 to 3, 4 to 7, ..., all dimensions but the last counted through in order) at most 4 rows name the same one
- route_weights: float32 [4, 128, 2], P(None, ('dp', 'tensor')), may hold values from 0.05 to 1
Outputs:
- new_master: float32 [3, 4, 1024, 2048], P(None, None, 'dp', 'tensor')
- new_moment_one: float32 [3, 4, 1024, 2048], P(None, None, 'dp', 'tensor')
- new_moment_two: float32 [3, 4, 1024, 2048], P(None, None, 'dp', 'tensor')
- served_weights: bfloat16 [3, 4096, 2048], P(None, 'dp')
- decoded: bfloat16 [4, 128, 2048], P(None, ('dp', 'tensor'))
Inputs may be any that keep to these rules, and one draw needn't show every extreme that they name: `expert_ids`: A row names 2 different experts; in each step the 4 rows of one device name one expert at most 4 times.
All inputs are finite; a program needn't handle non-finite values.
Results may differ from a plain program's by a relative error of at most 0.0067.
Values may be sent and summed in bfloat16 or wider, within the bound.
No kernel may reach another device: no remote copies, remote signals or barrier semaphores. Data moves between devices by JAX's collectives and lax.ppermute only.
A program may use at most 64 MiB of HBM per device.

v0:
```python
import math

import jax
import jax.numpy as jnp
from jax import lax
from jax.experimental import pallas as pl
from jax.experimental.pallas import tpu as pltpu
from jax.sharding import PartitionSpec as P


beta_one = 0.9
beta_two = 0.95
learn_rate = 0.02
decay_rate = 0.1
adam_eps = 1e-08
step_count = 10
norm_eps = 1e-06
lanes = 128
half = lanes // 2
megabyte = 1 << 20
kind_spans = (range(0, 3),)


def adam_update(master, moment_one, moment_two, gradients, clip_factor):
    scaled = gradients.astype(jnp.float32) * clip_factor
    first_moment = beta_one * moment_one + (1.0 - beta_one) * scaled
    second = beta_two * moment_two + (1.0 - beta_two) * scaled * scaled
    first_fix = 1.0 - beta_one**step_count
    second_fix = 1.0 - beta_two**step_count
    update = first_moment / first_fix / (jnp.sqrt(second / second_fix) + adam_eps)
    return (master - learn_rate * (update + decay_rate * master), first_moment, second)


def exchange(value, offset, member_count):
    return lax.ppermute(value, "dp", [(i, i ^ offset) for i in range(member_count)])


def stage_offsets(member_count):
    bits = member_count.bit_length() - 1
    assert 1 << bits == member_count
    pair = bits % 2
    return (pair, [[k << b for k in range(4)] for b in range(pair, bits, 2)])


hbm = pl.BlockSpec(memory_space=pltpu.HBM)
vmem = pl.BlockSpec(memory_space=pltpu.VMEM)


def call(kernel, out_shape, limit=24, **options):
    return pl.pallas_call(
        kernel,
        out_shape=out_shape,
        compiler_params=pltpu.CompilerParams(vmem_limit_bytes=limit * megabyte),
        **options,
    )


def prepare(gradients, hidden_in, norm_gain, expert_ids, route_weights, receivers):
    steps, row_count, model_width = hidden_in.shape
    top_count = expert_ids.shape[2]
    flat = gradients.reshape(-1, gradients.shape[-1])
    chunks = 6
    extent = flat.shape[0] // chunks

    def kernel(*refs):
        values, sources, sums, out, buffer = refs[0], refs[1:5], refs[5], refs[6], refs[7]
        buffers, done, arrived = refs[8:12], refs[12], refs[13]
        copies = [
            pltpu.make_async_copy(source, target, done.at[i])
            for i, (source, target) in enumerate(zip(sources, buffers))
        ]
        reads = [
            pltpu.make_async_copy(
                values.at[pl.ds(i * extent, extent)], buffer.at[i], arrived.at[i]
            )
            for i in range(chunks)
        ]
        for copy in copies + reads:
            copy.start()
        for copy in copies:
            copy.wait()
        hidden, gain, ids, gates = buffers
        rows = jnp.concatenate([hidden[s].astype(jnp.float32) for s in range(steps)], axis=0)
        factor = lax.rsqrt(jnp.mean(rows * rows, axis=1, keepdims=True) + norm_eps)
        out[:, :model_width] = (rows * factor * gain[...]).astype(jnp.bfloat16)
        lane = lax.rem(lax.broadcasted_iota(jnp.int32, (row_count, lanes), 1), half)
        diagonal = lax.broadcasted_iota(
            jnp.int32, (row_count, row_count), 0
        ) == lax.broadcasted_iota(jnp.int32, (row_count, row_count), 1)
        parts = []
        for s in range(steps):
            shares = gates[s] / jnp.sum(gates[s], axis=0, keepdims=True)
            mixed = jnp.zeros((row_count, lanes), jnp.float32)
            for k in range(top_count):
                named = jnp.where(diagonal, ids[s][k : k + 1], 0)
                share = jnp.where(diagonal, shares[k : k + 1], 0.0)
                mixed = mixed + jnp.where(
                    lane == jnp.sum(named, axis=1, keepdims=True),
                    jnp.sum(share, axis=1, keepdims=True),
                    0.0,
                )
            parts.append(mixed)
        combine = jnp.concatenate(parts, axis=0)
        lane = lax.broadcasted_iota(jnp.int32, combine.shape, 1)
        high = combine.astype(jnp.bfloat16).astype(jnp.float32)
        out[:, model_width:] = jnp.where(lane < half, high, combine - high).astype(jnp.bfloat16)
        total = jnp.zeros((8, flat.shape[1]), jnp.float32)
        for i, read in enumerate(reads):
            read.wait()
            widened = buffer[i].astype(jnp.float32)
            total = total + jnp.sum((widened * widened).reshape(-1, *total.shape), axis=0)
        sums[...] = jnp.full(sums.shape, jnp.sum(total), jnp.float32)

    arrays = (
        hidden_in,
        norm_gain.reshape(1, model_width),
        expert_ids.transpose(0, 2, 1),
        route_weights.transpose(0, 2, 1),
    )
    return call(
        kernel,
        (
            jax.ShapeDtypeStruct((receivers, 1, lanes), jnp.float32),
            jax.ShapeDtypeStruct((steps * row_count, model_width + lanes), jnp.bfloat16),
        ),
        limit=60,
        in_specs=[hbm] * 5,
        scratch_shapes=[pltpu.VMEM((chunks, extent, flat.shape[1]), flat.dtype)]
        + [pltpu.VMEM(array.shape, array.dtype) for array in arrays]
        + [pltpu.SemaphoreType.DMA((4,)), pltpu.SemaphoreType.DMA((chunks,))],
    )(flat, *arrays)


def expert_parts(row_blocks, weight_sets, hidden_total):
    expert_count, local_units, model_width = weight_sets[0][0].shape[1:]
    block_rows = row_blocks[0].shape[0]
    block_count, set_count, piece_count = len(row_blocks), len(weight_sets), len(weight_sets[0])
    pieces = [piece for weights in weight_sets for piece in weights]
    where = [(i, k) for i, piece in enumerate(weight_sets[0]) for k in range(piece.shape[0])]
    set_units = expert_count * local_units
    scale = 1.0 / math.sqrt(model_width)
    contract = (((1,), (1,)), ((), ()))

    def kernel(*refs):
        blocks, refs = refs[:block_count], refs[block_count:]
        held, outs = refs[: piece_count * set_count], refs[piece_count * set_count :]
        inputs = jnp.concatenate([b[...] for b in blocks], axis=0)
        rows, packed = inputs[:, :model_width], inputs[:, model_width:]

        def matrix(which):
            piece, kind = where[which]
            return jnp.concatenate(
                [
                    held[member * piece_count + piece][kind].reshape(set_units, model_width)
                    for member in range(set_count)
                ],
                axis=0,
            )

        units = set_count * set_units
        lane = lax.broadcasted_iota(jnp.int32, (lanes, units), 0)
        unit = lax.broadcasted_iota(jnp.int32, (lanes, units), 1)
        owner = lax.rem(unit, set_units) // local_units
        spread = (lax.rem(lane, half) == owner).astype(jnp.bfloat16)
        mix = jnp.dot(packed, spread, preferred_element_type=jnp.float32)
        gate = lax.dot_general(rows, matrix(0), contract, preferred_element_type=jnp.float32)
        up = lax.dot_general(rows, matrix(1), contract, preferred_element_type=jnp.float32)
        gate = gate * scale
        active = (gate / (1.0 + jnp.exp(-gate)) * (up * scale) * mix).astype(jnp.bfloat16)
        result = jnp.dot(active, matrix(2), preferred_element_type=jnp.float32)
        result = result * (1.0 / math.sqrt(hidden_total))
        for index, out in enumerate(outs):
            part = result[index * block_rows : (index + 1) * block_rows]
            out[...] = part.astype(out.dtype)

    shapes = [
        jax.ShapeDtypeStruct((block_rows, model_width), jnp.bfloat16 if b else jnp.float32)
        for b in range(block_count)
    ]
    return call(kernel, shapes, limit=40)(*row_blocks, *pieces)


def packing(strip_width):
    return max(1, 8 // strip_width)


def serve_step(master, moment_one, moment_two, gradients, sums, entries, strip_width, span):
    expert_count, local_units, local_width = master.shape[1:]
    first_kind, kinds = span.start, len(span)
    strips = local_units // strip_width
    pack = packing(strip_width)
    width = local_width // pack
    blocks = kinds * expert_count
    inputs = (master, moment_one, moment_two, gradients)
    first_scale = learn_rate / (1.0 - beta_one**step_count)
    second_scale = 1.0 / (1.0 - beta_two**step_count)

    def kernel(*refs):
        sources, shared, rounded, ordered = refs[:4], refs[4], refs[5], refs[6]
        buffers, packed, totals, got, put, summed = refs[7:11], *refs[11:16]
        fetch = pltpu.make_async_copy(shared, totals, summed.at[0])
        fetch.start()

        def place(b):
            return lax.div(b, expert_count), lax.rem(b, expert_count)

        def reads(b):
            k, e = place(b)
            return [
                pltpu.make_async_copy(source.at[first_kind + k, e], buffer.at[b], got.at[i, b])
                for i, (source, buffer) in enumerate(zip(sources, buffers))
            ]

        def write(b):
            k, e = place(b)
            return pltpu.make_async_copy(
                packed.at[b], ordered.at[pl.ds(e * strips, strips), k], put.at[b]
            )

        def issue(b, carry):
            for copy in reads(b):
                copy.start()
            return carry

        lax.fori_loop(0, blocks, issue, 0)
        fetch.wait()
        squares = jnp.sum(totals[:, :, :1])
        clip = jnp.minimum(1.0, lax.rsqrt(jnp.full((1, 1), squares) / entries + norm_eps))
        one_slope = clip * ((1.0 - beta_one) * first_scale)
        two_slope = clip * clip * ((1.0 - beta_two) * second_scale)

        def step(b, carry):
            for copy in reads(b):
                copy.wait()
            k, e = place(b)
            grad = buffers[3][b].astype(jnp.float32)
            top = buffers[1][b] * (beta_one * first_scale) + grad * one_slope
            square = buffers[2][b] * (beta_two * second_scale) + grad * grad * two_slope
            bottom = square * lax.rsqrt(square) + adam_eps
            new = buffers[0][b] * (1.0 - learn_rate * decay_rate) - top / bottom
            rounded[k, e] = new.astype(jnp.bfloat16)
            for t in range(strips):
                strip = new[t * strip_width : (t + 1) * strip_width]
                packed[b, t] = jnp.concatenate(
                    [strip[:, j * width : (j + 1) * width] for j in range(pack)], axis=0
                ).astype(jnp.bfloat16)
            write(b).start()
            return carry

        lax.fori_loop(0, blocks, step, 0)

        def finish(b, carry):
            write(b).wait()
            return carry

        lax.fori_loop(0, blocks, finish, 0)

    own = (local_units, local_width)
    return call(
        kernel,
        (
            jax.ShapeDtypeStruct((kinds,) + master.shape[1:], jnp.bfloat16),
            jax.ShapeDtypeStruct(
                (expert_count * strips, kinds, pack * strip_width, width), jnp.bfloat16
            ),
        ),
        limit=60,
        in_specs=[hbm] * 5,
        out_specs=(vmem, hbm),
        scratch_shapes=[pltpu.VMEM((blocks,) + own, array.dtype) for array in inputs]
        + [
            pltpu.VMEM((blocks, strips, pack * strip_width, width), jnp.bfloat16),
            pltpu.VMEM(sums.shape, sums.dtype),
            pltpu.SemaphoreType.DMA((4, blocks)),
            pltpu.SemaphoreType.DMA((blocks,)),
            pltpu.SemaphoreType.DMA((1,)),
        ],
    )(*inputs, sums)


def join_strips(owned, strip_width, first_kind, served):
    member_count, kinds, depth, width = owned.shape
    behind = [] if served is None else [served]
    pack = depth // strip_width
    split = 2
    members = member_count // split
    extent = members * strip_width

    def kernel(source, *refs):
        out, arrived, joined, got, put = refs[len(behind) :]

        def place(b):
            return lax.div(b, split), lax.rem(b, split)

        def read(b):
            k, h = place(b)
            return pltpu.make_async_copy(
                source.at[pl.ds(h * members, members), k], arrived.at[b], got.at[b]
            )

        def write(b):
            k, h = place(b)
            return pltpu.make_async_copy(
                joined.at[b], out.at[first_kind + k, pl.ds(h * extent, extent)], put.at[b]
            )

        for b in range(kinds * split):
            read(b).start()

        def step(b, carry):
            read(b).wait()
            for m in range(members // pack):
                group = [arrived[b, m * pack + g].astype(jnp.float32) for g in range(pack)]
                for j in range(pack):
                    joined[b, m * depth : (m + 1) * depth, j * width : (j + 1) * width] = (
                        jnp.concatenate(
                            [strip[j * strip_width : (j + 1) * strip_width] for strip in group],
                            axis=0,
                        ).astype(jnp.bfloat16)
                    )
            write(b).start()
            return carry

        lax.fori_loop(0, kinds * split, step, 0)
        for b in range(kinds * split):
            write(b).wait()

    return call(
        kernel,
        jax.ShapeDtypeStruct((3, member_count * strip_width, width * pack), jnp.bfloat16),
        input_output_aliases={1: 0} if behind else {},
        in_specs=[hbm] * (1 + len(behind)),
        out_specs=hbm,
        scratch_shapes=[
            pltpu.VMEM((kinds * split, members, depth, width), jnp.bfloat16),
            pltpu.VMEM((kinds * split, extent, width * pack), jnp.bfloat16),
            pltpu.SemaphoreType.DMA((kinds * split,)),
            pltpu.SemaphoreType.DMA((kinds * split,)),
        ],
    )(owned, *behind)


def per_device(
    master, moment_one, moment_two, gradients, norm_gain, hidden_in, expert_ids, route_weights
):
    slice_count = lax.axis_size("tensor")
    member_count = lax.axis_size("dp")
    expert_count = master.shape[1]
    local_units = master.shape[2]
    local_width = master.shape[3]
    hidden_total = local_units * member_count
    model_width = local_width * slice_count
    entries = 3 * expert_count * hidden_total * model_width
    pair, stages = stage_offsets(member_count)

    sums, gathered = prepare(
        gradients, hidden_in, norm_gain, expert_ids, route_weights, member_count
    )
    for place, offsets in enumerate(reversed(stages)):
        blocks = [gathered] + [exchange(gathered, k, member_count) for k in offsets[1:]]
        if place < len(stages) - 1:
            gathered = jnp.concatenate(blocks, axis=0)

    sums = lax.all_to_all(sums, "dp", split_axis=0, concat_axis=0, tiled=True)
    if slice_count > 1:
        sums = lax.psum(sums, "tensor")
    group_size = member_count // expert_count
    strip_width = local_units // group_size
    pack = packing(strip_width)
    weight_sets = [[] for _ in range(1 + pair)]
    arrived = []
    for span in kind_spans:
        whole, ordered = serve_step(
            master, moment_one, moment_two, gradients, sums, entries, strip_width, span
        )
        if slice_count > 1:
            whole = lax.all_gather(whole, "tensor", axis=3, tiled=True)
            ordered = whole.reshape(
                len(span), member_count, strip_width, pack, model_width // pack
            )
            ordered = ordered.transpose(1, 0, 3, 2, 4).reshape(
                member_count, len(span), pack * strip_width, model_width // pack
            )
        weight_sets[0].append(whole)
        if pair:
            weight_sets[1].append(exchange(whole, pair, member_count))
        arrived.append(
            lax.all_to_all(ordered, "dp", split_axis=0, concat_axis=0, tiled=True)
        )
    served = None
    for span, owned in zip(kind_spans, arrived):
        served = join_strips(owned, strip_width, span.start, served)

    squares = jnp.sum(sums[:, 0, 0])
    clip_factor = jnp.minimum(1.0, lax.rsqrt(squares / entries + norm_eps))
    new_master, new_one, new_two = adam_update(
        master, moment_one, moment_two, gradients, clip_factor
    )
    parts = expert_parts(blocks, weight_sets, hidden_total)
    for place, offsets in enumerate(stages):
        summed = parts[0]
        for index, k in enumerate(offsets[1:], 1):
            summed = summed + exchange(parts[index], k, member_count).astype(jnp.float32)
        if place < len(stages) - 1:
            extent = summed.shape[0] // len(offsets)
            pieces = [summed[i * extent : (i + 1) * extent] for i in range(len(offsets))]
            parts = pieces[:1] + [piece.astype(jnp.bfloat16) for piece in pieces[1:]]
    decoded = hidden_in.astype(jnp.float32) + summed.reshape(hidden_in.shape)
    return (new_master, new_one, new_two, served, decoded.astype(jnp.bfloat16))


def solution(mesh):
    in_specs = (
        P(None, None, "dp", "tensor"),
        P(None, None, "dp", "tensor"),
        P(None, None, "dp", "tensor"),
        P(None, None, "dp", "tensor"),
        P(),
        P(None, ("dp", "tensor"), None),
        P(None, ("dp", "tensor"), None),
        P(None, ("dp", "tensor"), None),
    )
    out_specs = (
        P(None, None, "dp", "tensor"),
        P(None, None, "dp", "tensor"),
        P(None, None, "dp", "tensor"),
        P(None, "dp", None),
        P(None, ("dp", "tensor"), None),
    )

    return jax.shard_map(
        per_device, mesh=mesh, in_specs=in_specs, out_specs=out_specs, check_vma=False
    )
```

profile of v0, /device:TPU:0, one launch (start us, length us, event | category | flops | bytes accessed | tf_op | source)
XLA Modules:
  0.0 95.2 jit_solution(2700387904724896159)
XLA Ops:
  0.6 2.3 %shard_map.119 = (f32[32,1,128]{2,1,0:T(1,128)}, bf16[16,2176]{1,0:T(8,128)(2,1)}) custom-call(bf16[384,2048]{1,0:T(8,128)(2,1)} %bitcast.4, bf16[4,4,2048]{2,1,0:T(4,128)(2,1)} %refs_1_.2, f32[1,2048]{1,0:T(1,128)} %bitcast.5, s32[4,2,4]{2,1,0:T(2,128)} %bitcast.6, f32[4,2,4]{2,1,0:T(2,128)} %bitcast.7), custom_call_target="tpu_custom_call" | custom-call | tf_op jit(solution)/shard_map/pallas_call | solution.py:120
  2.9 7.3 %all-to-all-start = ((f32[32,1,128]{2,1,0:T(1,128)}), f32[32,1,128]{2,1,0:T(1,128)S(1)}, u32[]{:S(2)}, u32[]{:S(2)}) async-start(f32[32,1,128]{2,1,0:T(1,128)} %get-tuple-element.13), calls=%async_computation | async-start | bytes 32768 | tf_op jit(solution)/shard_map/all_to_all | solution.py:364
  10.2 0.0 copy-start.5
  10.2 3.7 %collective-permute-start.2 = (bf16[16,2176]{1,0:T(8,128)(2,1)}, bf16[16,2176]{1,0:T(8,128)(2,1)S(1)}, u32[]{:S(2)}, u32[]{:S(2)}) collective-permute-start(bf16[16,2176]{1,0:T(8,128)(2,1)} %get-tuple-element.15), channel_id=1, source_target_pairs={{0,24},{1,25},{2,26},{3,27},{4,28},{5,29},{6,30},{7,31},{8,16},{9,... | collective-permute-start | bytes 208904 | tf_op jit(solution)/shard_map/ppermute | solution.py:35
  13.9 0.0 collective-permute-start.1
  13.9 0.8 collective-permute-start
  14.7 2.7 %all-to-all-done.refs_4_ = f32[32,1,128]{2,1,0:T(1,128)S(1)} async-done(((f32[32,1,128]{2,1,0:T(1,128)}), f32[32,1,128]{2,1,0:T(1,128)S(1)}, u32[]{:S(2)}, u32[]{:S(2)}) %all-to-all-start) | async-done | bytes 16416 | tf_op jit(solution)/shard_map/all_to_all | solution.py:364
  17.4 0.6 copy-done.3
  18.0 7.0 %shard_map.120 = (bf16[3,4,32,2048]{3,2,1,0:T(8,128)(2,1)}, bf16[32,3,8,1024]{3,2,1,0:T(8,128)(2,1)}) custom-call(f32[3,4,32,2048]{3,2,1,0:T(8,128)} %refs_0_.1, f32[3,4,32,2048]{3,2,1,0:T(8,128)} %refs_1_.3, f32[3,4,32,2048]{3,2,1,0:T(8,128)} %refs_2_.1, bf16[3,4,32,2048]{3,2,1,0:T(8,128)(2,1)} %refs_3_.1, f32[32,1,128]{2,1,0:T(1,128)} %copy-done.3), custom_call_target="tpu_custom_call" | custom-call | tf_op jit(solution)/shard_map/pallas_call | solution.py:259
  25.0 0.1 collective-permute-start.6
  25.1 0.0 copy-done.5
  25.1 0.0 collective-permute-done
  25.2 0.0 collective-permute-done.1
  25.2 0.0 collective-permute-done.2
  25.2 0.0 copy-start.4
  25.2 0.7 collective-permute-start.5
  25.9 1.3 %collective-permute-start.4 = (bf16[64,2176]{1,0:T(8,128)(2,1)S(1)}, bf16[64,2176]{1,0:T(8,128)(2,1)S(1)}, u32[]{:S(2)}, u32[]{:S(2)}) collective-permute-start(bf16[64,2176]{1,0:T(8,128)(2,1)S(1)} %constant_dynamic-update-slice_fusion.refs_0_), channel_id=1, source_target_pairs={{0,4},{1,5},{2,6},{3,7},{4,0},{5,1},{6,2},{7,3},{8,12},{9,13},{10,... | collective-permute-start | bytes 835592 | tf_op jit(solution)/shard_map/ppermute | solution.py:35
  27.3 1.5 %collective-permute-start.3 = (bf16[64,2176]{1,0:T(8,128)(2,1)S(1)}, bf16[64,2176]{1,0:T(8,128)(2,1)S(1)}, u32[]{:S(2)}, u32[]{:S(2)}) collective-permute-start(bf16[64,2176]{1,0:T(8,128)(2,1)S(1)} %constant_dynamic-update-slice_fusion.refs_0_), channel_id=1, source_target_pairs={{0,2},{1,3},{2,0},{3,1},{4,6},{5,7},{6,4},{7,5},{8,10},{9,11},{10,... | collective-permute-start | bytes 835592 | tf_op jit(solution)/shard_map/ppermute | solution.py:35
  28.8 7.0 %collective-permute-done.5.refs_3_ = bf16[64,2176]{1,0:T(8,128)(2,1)S(1)} collective-permute-done((bf16[64,2176]{1,0:T(8,128)(2,1)S(1)}, bf16[64,2176]{1,0:T(8,128)(2,1)S(1)}, u32[]{:S(2)}, u32[]{:S(2)}) %collective-permute-start.5) | collective-permute-done | bytes 278560 | tf_op jit(solution)/shard_map/ppermute | solution.py:35
  35.8 4.9 %collective-permute-done.4.refs_2_ = bf16[64,2176]{1,0:T(8,128)(2,1)S(1)} collective-permute-done((bf16[64,2176]{1,0:T(8,128)(2,1)S(1)}, bf16[64,2176]{1,0:T(8,128)(2,1)S(1)}, u32[]{:S(2)}, u32[]{:S(2)}) %collective-permute-start.4) | collective-permute-done | bytes 278560 | tf_op jit(solution)/shard_map/ppermute | solution.py:35
  40.7 0.0 collective-permute-done.3.refs_1_
  40.7 0.0 collective-permute-done.6.refs_5_
  40.7 1.4 %copy-done = bf16[3,4,32,2048]{3,2,1,0:T(8,128)(2,1)S(1)} copy-done((bf16[3,4,32,2048]{3,2,1,0:T(8,128)(2,1)S(1)}, bf16[3,4,32,2048]{3,2,1,0:T(8,128)(2,1)}, u32[]{:S(2)}) %copy-start) | copy-done | bytes 1572888
  42.1 1.1 %shard_map.122 = (f32[64,2048]{1,0:T(8,128)S(1)}, bf16[64,2048]{1,0:T(8,128)(2,1)S(1)}, bf16[64,2048]{1,0:T(8,128)(2,1)S(1)}, bf16[64,2048]{1,0:T(8,128)(2,1)S(1)}) custom-call(bf16[64,2176]{1,0:T(8,128)(2,1)S(1)} %constant_dynamic-update-slice_fusion.refs_0_, bf16[64,2176]{1,0:T(8,128)(2,1)S(1)} %collective-permute-done.3.refs_1_, ...), custom_call_target="tpu_custom_call" | custom-call | tf_op jit(solution)/shard_map/pallas_call | solution.py:180
  43.2 1.1 %collective-permute-start.7 = (bf16[64,2048]{1,0:T(8,128)(2,1)S(1)}, bf16[64,2048]{1,0:T(8,128)(2,1)S(1)}, u32[]{:S(2)}, u32[]{:S(2)}) collective-permute-start(bf16[64,2048]{1,0:T(8,128)(2,1)S(1)} %get-tuple-element.18), channel_id=1, source_target_pairs={{0,2},{1,3},{2,0},{3,1},{4,6},{5,7},{6,4},{7,5},{8,10},{9,11},{10,... | collective-permute-start | bytes 786440 | tf_op jit(solution)/shard_map/ppermute | solution.py:35
  44.3 0.7 collective-permute-start.8
  45.0 1.7 %collective-permute-start.9 = (bf16[64,2048]{1,0:T(8,128)(2,1)S(1)}, bf16[64,2048]{1,0:T(8,128)(2,1)}, u32[]{:S(2)}, u32[]{:S(2)}) collective-permute-start(bf16[64,2048]{1,0:T(8,128)(2,1)S(1)} %get-tuple-element.20), channel_id=1, source_target_pairs={{0,6},{1,7},{2,4},{3,5},{4,2},{5,3},{6,0},{7,1},{8,14},{9,15},{10,... | collective-permute-start | bytes 786440 | tf_op jit(solution)/shard_map/ppermute | solution.py:35
  46.8 3.0 %all-to-all-start.1 = ((bf16[32,3,8,1024]{3,2,1,0:T(8,128)(2,1)}), bf16[32,3,8,1024]{3,2,1,0:T(8,128)(2,1)S(1)}, u32[]{:S(2)}, u32[]{:S(2)}) async-start(bf16[32,3,8,1024]{3,2,1,0:T(8,128)(2,1)} %get-tuple-element.14), calls=%async_computation.1 | async-start | bytes 3145728 | tf_op jit(solution)/shard_map/all_to_all | solution.py:388
  49.8 0.0 copy-done.4
  49.8 0.6 slice_reduce_fusion
  51.1 0.0 copy-start.1
  51.1 1.3 %collective-permute-done.7 = bf16[64,2048]{1,0:T(8,128)(2,1)S(1)} collective-permute-done((bf16[64,2048]{1,0:T(8,128)(2,1)S(1)}, bf16[64,2048]{1,0:T(8,128)(2,1)S(1)}, u32[]{:S(2)}, u32[]{:S(2)}) %collective-permute-start.7) | collective-permute-done | bytes 262176 | tf_op jit(solution)/shard_map/ppermute | solution.py:35
  52.5 7.3 %collective-permute-done.8 = bf16[64,2048]{1,0:T(8,128)(2,1)S(1)} collective-permute-done((bf16[64,2048]{1,0:T(8,128)(2,1)S(1)}, bf16[64,2048]{1,0:T(8,128)(2,1)S(1)}, u32[]{:S(2)}, u32[]{:S(2)}) %collective-permute-start.8) | collective-permute-done | bytes 262176 | tf_op jit(solution)/shard_map/ppermute | solution.py:35
  59.7 5.3 %collective-permute-done.9 = bf16[64,2048]{1,0:T(8,128)(2,1)} collective-permute-done((bf16[64,2048]{1,0:T(8,128)(2,1)S(1)}, bf16[64,2048]{1,0:T(8,128)(2,1)}, u32[]{:S(2)}, u32[]{:S(2)}) %collective-permute-start.9) | collective-permute-done | bytes 262176 | tf_op jit(solution)/shard_map/ppermute | solution.py:35
  65.0 1.1 %fusion.3 = (bf16[64,2048]{1,0:T(8,128)(2,1)S(1)}, f32[64,2048]{1,0:T(8,128)S(1)}) fusion(bf16[64,2048]{1,0:T(8,128)(2,1)} %collective-permute-done.9, bf16[64,2048]{1,0:T(8,128)(2,1)S(1)} %collective-permute-done.8, f32[64,2048]{1,0:T(8,128)S(1)} %get-tuple-element.17, bf16[64,2048]{1,0:T(8,128)(2,1)S(1)} %collective-permute-done.7), kind=kLoop, calls=%fused_computation.15 | loop fusion | flops 917504 | bytes 2097152 | tf_op jit(solution)/shard_map/convert.2
  66.1 0.1 collective-permute-start.10
  66.2 0.1 collective-permute-start.12
  66.3 0.0 copy-start.2
  66.3 3.4 %collective-permute-start.11 = (bf16[16,2048]{1,0:T(8,128)(2,1)S(1)}, bf16[16,2048]{1,0:T(8,128)(2,1)S(1)}, u32[]{:S(2)}, u32[]{:S(2)}) collective-permute-start(bf16[16,2048]{1,0:T(8,128)(2,1)S(1)} %get-tuple-element.28), channel_id=1, source_target_pairs={{0,16},{1,17},{2,18},{3,19},{4,20},{5,21},{6,22},{7,23},{8,24},{9,... | collective-permute-start | bytes 196616 | tf_op jit(solution)/shard_map/ppermute | solution.py:35
  69.7 0.0 copy-done.1
  69.7 7.3 %multiply_subtract_fusion = (f32[3,4,32,2048]{3,2,1,0:T(8,128)}, f32[3,4,32,2048]{3,2,1,0:T(8,128)}, f32[3,4,32,2048]{3,2,1,0:T(8,128)}) fusion(f32[3,4,32,2048]{3,2,1,0:T(8,128)} %refs_0_.1, f32[]{:T(128)S(6)} %min_shard_map.3, bf16[3,4,32,2048]{3,2,1,0:T(8,128)(2,1)S(1)} %copy-done.1, f32[3,4,32,2048]{3,2,1,0:T(8,128)} %refs_1_.3, f32[3,4,32,2048]{3,2,1,0:T(8,128)} %refs_2_.1), kind=kLoop, calls=%fused_computation.2 | loop fusion | flops 13369344 | bytes 20447236 | tf_op jit(solution)/shard_map/sub | solution.py:31
  77.0 0.9 collective-permute-done.10
  77.9 5.2 %collective-permute-done.12 = bf16[16,2048]{1,0:T(8,128)(2,1)S(1)} collective-permute-done((bf16[16,2048]{1,0:T(8,128)(2,1)S(1)}, bf16[16,2048]{1,0:T(8,128)(2,1)S(1)}, u32[]{:S(2)}, u32[]{:S(2)}) %collective-permute-start.12) | collective-permute-done | bytes 65568 | tf_op jit(solution)/shard_map/ppermute | solution.py:35
  83.2 9.8 %collective-permute-done.11 = bf16[16,2048]{1,0:T(8,128)(2,1)S(1)} collective-permute-done((bf16[16,2048]{1,0:T(8,128)(2,1)S(1)}, bf16[16,2048]{1,0:T(8,128)(2,1)S(1)}, u32[]{:S(2)}, u32[]{:S(2)}) %collective-permute-start.11) | collective-permute-done | bytes 65568 | tf_op jit(solution)/shard_map/ppermute | solution.py:35
  93.1 0.0 copy-done.2
  93.1 0.7 add_convert_fusion
  93.8 0.0 all-to-all-done.1.source
  93.8 1.4 %shard_map.121 = bf16[3,128,2048]{2,1,0:T(8,128)(2,1)} custom-call(bf16[32,3,8,1024]{3,2,1,0:T(8,128)(2,1)S(1)} %all-to-all-done.1.source), custom_call_target="tpu_custom_call" | custom-call | tf_op jit(solution)/shard_map/pallas_call | solution.py:328
  (9 shorter events, 0.1 us)
Async XLA Ops:
  2.9 14.5 %all-to-all-start = ((f32[32,1,128]{2,1,0:T(1,128)}), f32[32,1,128]{2,1,0:T(1,128)S(1)}, u32[]{:S(2)}, u32[]{:S(2)}) async-start(f32[32,1,128]{2,1,0:T(1,128)} %get-tuple-element.13), calls=%async_computation | async-start | bytes 32768 | tf_op jit(solution)/shard_map/all_to_all | solution.py:364
  10.2 14.9 %copy-start.5 = (bf16[16,2176]{1,0:T(8,128)(2,1)S(1)}, bf16[16,2176]{1,0:T(8,128)(2,1)}, u32[]{:S(2)}) copy-start(bf16[16,2176]{1,0:T(8,128)(2,1)} %get-tuple-element.15) | copy-start | bytes 208900
  10.2 15.0 %collective-permute-start.2 = (bf16[16,2176]{1,0:T(8,128)(2,1)}, bf16[16,2176]{1,0:T(8,128)(2,1)S(1)}, u32[]{:S(2)}, u32[]{:S(2)}) collective-permute-start(bf16[16,2176]{1,0:T(8,128)(2,1)} %get-tuple-element.15), channel_id=1, source_target_pairs={{0,24},{1,25},{2,26},{3,27},{4,28},{5,29},{6,30},{7,31},{8,16},{9,... | collective-permute-start | bytes 208904 | tf_op jit(solution)/shard_map/ppermute | solution.py:35
  13.9 11.2 %collective-permute-start.1 = (bf16[16,2176]{1,0:T(8,128)(2,1)}, bf16[16,2176]{1,0:T(8,128)(2,1)S(1)}, u32[]{:S(2)}, u32[]{:S(2)}) collective-permute-start(bf16[16,2176]{1,0:T(8,128)(2,1)} %get-tuple-element.15), channel_id=1, source_target_pairs={{0,16},{1,17},{2,18},{3,19},{4,20},{5,21},{6,22},{7,23},{8,24},{9,... | collective-permute-start | bytes 208904 | tf_op jit(solution)/shard_map/ppermute | solution.py:35
  13.9 11.2 %collective-permute-start = (bf16[16,2176]{1,0:T(8,128)(2,1)}, bf16[16,2176]{1,0:T(8,128)(2,1)S(1)}, u32[]{:S(2)}, u32[]{:S(2)}) collective-permute-start(bf16[16,2176]{1,0:T(8,128)(2,1)} %get-tuple-element.15), channel_id=1, source_target_pairs={{0,8},{1,9},{2,10},{3,11},{4,12},{5,13},{6,14},{7,15},{8,0},{9,1},... | collective-permute-start | bytes 208904 | tf_op jit(solution)/shard_map/ppermute | solution.py:35
  17.4 0.6 copy-start.3
  25.0 15.6 %collective-permute-start.6 = (bf16[3,4,32,2048]{3,2,1,0:T(8,128)(2,1)}, bf16[3,4,32,2048]{3,2,1,0:T(8,128)(2,1)S(1)}, u32[]{:S(2)}, u32[]{:S(2)}) collective-permute-start(bf16[3,4,32,2048]{3,2,1,0:T(8,128)(2,1)} %get-tuple-element.16.refs_4_), channel_id=1, source_target_pairs={{0,1},{1,0},{2,3},{3,2},{4,5},{5,4},{6,7},{7,6},{8,9},{9,8},{10,11... | collective-permute-start | bytes 4718600 | tf_op jit(solution)/shard_map/ppermute | solution.py:35
  25.2 24.6 %copy-start.4 = (f32[32,1,128]{2,1,0:T(1,128)S(1)}, f32[32,1,128]{2,1,0:T(1,128)}, u32[]{:S(2)}) copy-start(f32[32,1,128]{2,1,0:T(1,128)} %copy-done.3) | copy-start | bytes 49156
  25.2 10.5 %collective-permute-start.5 = (bf16[64,2176]{1,0:T(8,128)(2,1)S(1)}, bf16[64,2176]{1,0:T(8,128)(2,1)S(1)}, u32[]{:S(2)}, u32[]{:S(2)}) collective-permute-start(bf16[64,2176]{1,0:T(8,128)(2,1)S(1)} %constant_dynamic-update-slice_fusion.refs_0_), channel_id=1, source_target_pairs={{0,6},{1,7},{2,4},{3,5},{4,2},{5,3},{6,0},{7,1},{8,14},{9,15},{10,... | collective-permute-start | bytes 835592 | tf_op jit(solution)/shard_map/ppermute | solution.py:35
  25.9 14.7 %collective-permute-start.4 = (bf16[64,2176]{1,0:T(8,128)(2,1)S(1)}, bf16[64,2176]{1,0:T(8,128)(2,1)S(1)}, u32[]{:S(2)}, u32[]{:S(2)}) collective-permute-start(bf16[64,2176]{1,0:T(8,128)(2,1)S(1)} %constant_dynamic-update-slice_fusion.refs_0_), channel_id=1, source_target_pairs={{0,4},{1,5},{2,6},{3,7},{4,0},{5,1},{6,2},{7,3},{8,12},{9,13},{10,... | collective-permute-start | bytes 835592 | tf_op jit(solution)/shard_map/ppermute | solution.py:35
  27.3 13.4 %collective-permute-start.3 = (bf16[64,2176]{1,0:T(8,128)(2,1)S(1)}, bf16[64,2176]{1,0:T(8,128)(2,1)S(1)}, u32[]{:S(2)}, u32[]{:S(2)}) collective-permute-start(bf16[64,2176]{1,0:T(8,128)(2,1)S(1)} %constant_dynamic-update-slice_fusion.refs_0_), channel_id=1, source_target_pairs={{0,2},{1,3},{2,0},{3,1},{4,6},{5,7},{6,4},{7,5},{8,10},{9,11},{10,... | collective-permute-start | bytes 835592 | tf_op jit(solution)/shard_map/ppermute | solution.py:35
  40.7 1.4 %copy-start = (bf16[3,4,32,2048]{3,2,1,0:T(8,128)(2,1)S(1)}, bf16[3,4,32,2048]{3,2,1,0:T(8,128)(2,1)}, u32[]{:S(2)}) copy-start(bf16[3,4,32,2048]{3,2,1,0:T(8,128)(2,1)} %get-tuple-element.16.refs_4_) | copy-start | bytes 4718596
  43.2 9.2 %collective-permute-start.7 = (bf16[64,2048]{1,0:T(8,128)(2,1)S(1)}, bf16[64,2048]{1,0:T(8,128)(2,1)S(1)}, u32[]{:S(2)}, u32[]{:S(2)}) collective-permute-start(bf16[64,2048]{1,0:T(8,128)(2,1)S(1)} %get-tuple-element.18), channel_id=1, source_target_pairs={{0,2},{1,3},{2,0},{3,1},{4,6},{5,7},{6,4},{7,5},{8,10},{9,11},{10,... | collective-permute-start | bytes 786440 | tf_op jit(solution)/shard_map/ppermute | solution.py:35
  44.3 15.4 %collective-permute-start.8 = (bf16[64,2048]{1,0:T(8,128)(2,1)S(1)}, bf16[64,2048]{1,0:T(8,128)(2,1)S(1)}, u32[]{:S(2)}, u32[]{:S(2)}) collective-permute-start(bf16[64,2048]{1,0:T(8,128)(2,1)S(1)} %get-tuple-element.19), channel_id=1, source_target_pairs={{0,4},{1,5},{2,6},{3,7},{4,0},{5,1},{6,2},{7,3},{8,12},{9,13},{10,... | collective-permute-start | bytes 786440 | tf_op jit(solution)/shard_map/ppermute | solution.py:35
  45.0 20.0 %collective-permute-start.9 = (bf16[64,2048]{1,0:T(8,128)(2,1)S(1)}, bf16[64,2048]{1,0:T(8,128)(2,1)}, u32[]{:S(2)}, u32[]{:S(2)}) collective-permute-start(bf16[64,2048]{1,0:T(8,128)(2,1)S(1)} %get-tuple-element.20), channel_id=1, source_target_pairs={{0,6},{1,7},{2,4},{3,5},{4,2},{5,3},{6,0},{7,1},{8,14},{9,15},{10,... | collective-permute-start | bytes 786440 | tf_op jit(solution)/shard_map/ppermute | solution.py:35
  46.8 47.0 %all-to-all-start.1 = ((bf16[32,3,8,1024]{3,2,1,0:T(8,128)(2,1)}), bf16[32,3,8,1024]{3,2,1,0:T(8,128)(2,1)S(1)}, u32[]{:S(2)}, u32[]{:S(2)}) async-start(bf16[32,3,8,1024]{3,2,1,0:T(8,128)(2,1)} %get-tuple-element.14), calls=%async_computation.1 | async-start | bytes 3145728 | tf_op jit(solution)/shard_map/all_to_all | solution.py:388
  51.1 18.6 %copy-start.1 = (bf16[3,4,32,2048]{3,2,1,0:T(8,128)(2,1)S(1)}, bf16[3,4,32,2048]{3,2,1,0:T(8,128)(2,1)}, u32[]{:S(2)}) copy-start(bf16[3,4,32,2048]{3,2,1,0:T(8,128)(2,1)} %refs_3_.1) | copy-start | bytes 4718596
  66.1 11.8 %collective-permute-start.10 = (bf16[16,2048]{1,0:T(8,128)(2,1)S(1)}, bf16[16,2048]{1,0:T(8,128)(2,1)S(1)}, u32[]{:S(2)}, u32[]{:S(2)}) collective-permute-start(bf16[16,2048]{1,0:T(8,128)(2,1)S(1)} %get-tuple-element.26), channel_id=1, source_target_pairs={{0,8},{1,9},{2,10},{3,11},{4,12},{5,13},{6,14},{7,15},{8,0},{9,1},... | collective-permute-start | bytes 196616 | tf_op jit(solution)/shard_map/ppermute | solution.py:35
  66.2 16.9 %collective-permute-start.12 = (bf16[16,2048]{1,0:T(8,128)(2,1)S(1)}, bf16[16,2048]{1,0:T(8,128)(2,1)S(1)}, u32[]{:S(2)}, u32[]{:S(2)}) collective-permute-start(bf16[16,2048]{1,0:T(8,128)(2,1)S(1)} %get-tuple-element.27), channel_id=1, source_target_pairs={{0,24},{1,25},{2,26},{3,27},{4,28},{5,29},{6,30},{7,31},{8,16},{9,... | collective-permute-start | bytes 196616 | tf_op jit(solution)/shard_map/ppermute | solution.py:35
  66.3 26.8 %copy-start.2 = (bf16[4,4,2048]{2,1,0:T(4,128)(2,1)S(1)}, bf16[4,4,2048]{2,1,0:T(4,128)(2,1)}, u32[]{:S(2)}) copy-start(bf16[4,4,2048]{2,1,0:T(4,128)(2,1)} %refs_1_.2) | copy-start | bytes 196612
  66.3 26.7 %collective-permute-start.11 = (bf16[16,2048]{1,0:T(8,128)(2,1)S(1)}, bf16[16,2048]{1,0:T(8,128)(2,1)S(1)}, u32[]{:S(2)}, u32[]{:S(2)}) collective-permute-start(bf16[16,2048]{1,0:T(8,128)(2,1)S(1)} %get-tuple-element.28), channel_id=1, source_target_pairs={{0,16},{1,17},{2,18},{3,19},{4,20},{5,21},{6,22},{7,23},{8,24},{9,... | collective-permute-start | bytes 196616 | tf_op jit(solution)/shard_map/ppermute | solution.py:35
where the time goes:
time: 95.5 us; the launch traced here: 95.2 us
  waiting for transfers between devices  44.5 us (47%)
  starting transfers between devices  25.5 us (27%)
  Pallas kernels  11.8 us (12%)
  other arithmetic  9.7 us (10%)
  local copies, waits for them, and re-layouts  2.14 us (2%)
  between operations  1.52 us (2%)
    ppermute x13, waiting for transfers between devices, exchange(): lax.ppermute(value, 'dp', [(i, i ^ offset) for i in range(member_count)])  41.8 us
    ppermute x13, starting transfers between devices, exchange(): lax.ppermute(value, 'dp', [(i, i ^ offset) for i in range(member_count)])  15.2 us
    all_to_all x1, starting transfers between devices, per_device(): sums = lax.all_to_all(sums, 'dp', split_axis=0, concat_axis=0, tiled=True)  7.33 us
    sub x1, other arithmetic, adam_update(): master - learn_rate * (update + decay_rate * master)  7.3 us
    pallas_call x1, Pallas kernels, serve_step(): call(kernel, (jax.ShapeDtypeStruct((kinds,) + master.shape[1:], jnp.bfloa...  7.02 us
    all_to_all x1, starting transfers between devices, per_device(): lax.all_to_all(ordered, 'dp', split_axis=0, concat_axis=0, tiled=True)  3 us
    all_to_all x1, waiting for transfers between devices, per_device(): sums = lax.all_to_all(sums, 'dp', split_axis=0, concat_axis=0, tiled=True)  2.71 us
    pallas_call x1, Pallas kernels, prepare(): call(kernel, (jax.ShapeDtypeStruct((receivers, 1, lanes), jnp.float32), j...  2.25 us
  transfers between devices with their start and end apart: 15, of which 9 were waited for; matrix products, arithmetic and copies ran while one was open for 10% of the time, Pallas kernels for 7%

commit v1 on v0

--- a/solution.py
+++ b/solution.py
@@ -197,7 +197,7 @@
 
     def kernel(*refs):
         sources, shared, rounded, ordered = refs[:4], refs[4], refs[5], refs[6]
-        buffers, packed, totals, got, put, summed = refs[7:11], *refs[11:16]
+        buffers, packed, plain, totals, got, put, summed = refs[7:11], *refs[11:17]
         fetch = pltpu.make_async_copy(shared, totals, summed.at[0])
         fetch.start()
 
@@ -211,11 +211,14 @@
                 for i, (source, buffer) in enumerate(zip(sources, buffers))
             ]
 
-        def write(b):
+        def writes(b):
             k, e = place(b)
-            return pltpu.make_async_copy(
-                packed.at[b], ordered.at[pl.ds(e * strips, strips), k], put.at[b]
-            )
+            return [
+                pltpu.make_async_copy(
+                    packed.at[b], ordered.at[pl.ds(e * strips, strips), k], put.at[0, b]
+                ),
+                pltpu.make_async_copy(plain.at[b], rounded.at[k, e], put.at[1, b]),
+            ]
 
         def issue(b, carry):
             for copy in reads(b):
@@ -238,19 +241,21 @@
             square = buffers[2][b] * (beta_two * second_scale) + grad * grad * two_slope
             bottom = square * lax.rsqrt(square) + adam_eps
             new = buffers[0][b] * (1.0 - learn_rate * decay_rate) - top / bottom
-            rounded[k, e] = new.astype(jnp.bfloat16)
+            plain[b] = new.astype(jnp.bfloat16)
             for t in range(strips):
                 strip = new[t * strip_width : (t + 1) * strip_width]
                 packed[b, t] = jnp.concatenate(
                     [strip[:, j * width : (j + 1) * width] for j in range(pack)], axis=0
                 ).astype(jnp.bfloat16)
-            write(b).start()
+            for copy in writes(b):
+                copy.start()
             return carry
 
         lax.fori_loop(0, blocks, step, 0)
 
         def finish(b, carry):
-            write(b).wait()
+            for copy in writes(b):
+                copy.wait()
             return carry
 
         lax.fori_loop(0, blocks, finish, 0)
@@ -266,13 +271,14 @@
         ),
         limit=60,
         in_specs=[hbm] * 5,
-        out_specs=(vmem, hbm),
+        out_specs=(hbm, hbm),
         scratch_shapes=[pltpu.VMEM((blocks,) + own, array.dtype) for array in inputs]
         + [
             pltpu.VMEM((blocks, strips, pack * strip_width, width), jnp.bfloat16),
+            pltpu.VMEM((blocks,) + own, jnp.bfloat16),
             pltpu.VMEM(sums.shape, sums.dtype),
             pltpu.SemaphoreType.DMA((4, blocks)),
-            pltpu.SemaphoreType.DMA((blocks,)),
+            pltpu.SemaphoreType.DMA((2, blocks)),
             pltpu.SemaphoreType.DMA((1,)),
         ],
     )(*inputs, sums)
@@ -357,7 +363,8 @@
         gradients, hidden_in, norm_gain, expert_ids, route_weights, member_count
     )
     for place, offsets in enumerate(reversed(stages)):
-        blocks = [gathered] + [exchange(gathered, k, member_count) for k in offsets[1:]]
+        others = [exchange(gathered, k, member_count) for k in reversed(offsets[1:])]
+        blocks = [gathered] + others[::-1]
         if place < len(stages) - 1:
             gathered = jnp.concatenate(blocks, axis=0)
 
@@ -399,7 +406,7 @@
     parts = expert_parts(blocks, weight_sets, hidden_total)
     for place, offsets in enumerate(stages):
         summed = parts[0]
-        for index, k in enumerate(offsets[1:], 1):
+        for index, k in reversed(list(enumerate(offsets[1:], 1))):
             summed = summed + exchange(parts[index], k, member_count).astype(jnp.float32)
         if place < len(stages) - 1:
             extent = summed.shape[0] // len(offsets)

time: 95.5 us -> 94.9 us (level)
  transfers between devices with their start and end apart: 15 -> 15, of which waited for: 9 -> 8; matrix products, arithmetic and copies ran while one was open for 10% -> 10% of each run, Pallas kernels for 7% -> 7%
where the time goes in v1:
time: 94.9 us; the launch traced here: 94.5 us
  waiting for transfers between devices  43.6 us (46%)
  starting transfers between devices  26.4 us (28%)
  Pallas kernels  11.2 us (12%)
  other arithmetic  9.7 us (10%)
  local copies, waits for them, and re-layouts  2.14 us (2%)
  between operations  1.52 us (2%)
    ppermute x13, waiting for transfers between devices, exchange(): lax.ppermute(value, 'dp', [(i, i ^ offset) for i in range(member_count)])  40.9 us
    ppermute x13, starting transfers between devices, exchange(): lax.ppermute(value, 'dp', [(i, i ^ offset) for i in range(member_count)])  16.1 us
    all_to_all x1, starting transfers between devices, per_device(): sums = lax.all_to_all(sums, 'dp', split_axis=0, concat_axis=0, tiled=True)  7.33 us
    sub x1, other arithmetic, adam_update(): master - learn_rate * (update + decay_rate * master)  7.3 us
    pallas_call x1, Pallas kernels, serve_step(): call(kernel, (jax.ShapeDtypeStruct((kinds,) + master.shape[1:], jnp.bfloa...  6.38 us
    all_to_all x1, starting transfers between devices, per_device(): lax.all_to_all(ordered, 'dp', split_axis=0, concat_axis=0, tiled=True)  2.99 us
    all_to_all x1, waiting for transfers between devices, per_device(): sums = lax.all_to_all(sums, 'dp', split_axis=0, concat_axis=0, tiled=True)  2.71 us
    pallas_call x1, Pallas kernels, prepare(): call(kernel, (jax.ShapeDtypeStruct((receivers, 1, lanes), jnp.float32), j...  2.25 us
  transfers between devices with their start and end apart: 15, of which 8 were waited for; matrix products, arithmetic and copies ran while one was open for 10% of the time, Pallas kernels for 7%

profile of v1, /device:TPU:0, one launch (start us, length us, event | category | flops | bytes accessed | tf_op | source)
XLA Modules:
  0.0 94.5 jit_solution(3092343755447407209)
XLA Ops:
  0.6 2.3 %shard_map.119 = (f32[32,1,128]{2,1,0:T(1,128)}, bf16[16,2176]{1,0:T(8,128)(2,1)}) custom-call(bf16[384,2048]{1,0:T(8,128)(2,1)} %bitcast.4, bf16[4,4,2048]{2,1,0:T(4,128)(2,1)} %refs_1_.2, f32[1,2048]{1,0:T(1,128)} %bitcast.5, s32[4,2,4]{2,1,0:T(2,128)} %bitcast.6, f32[4,2,4]{2,1,0:T(2,128)} %bitcast.7), custom_call_target="tpu_custom_call" | custom-call | tf_op jit(solution)/shard_map/pallas_call | solution.py:120
  2.9 7.3 %all-to-all-start = ((f32[32,1,128]{2,1,0:T(1,128)}), f32[32,1,128]{2,1,0:T(1,128)S(1)}, u32[]{:S(2)}, u32[]{:S(2)}) async-start(f32[32,1,128]{2,1,0:T(1,128)} %get-tuple-element.13), calls=%async_computation | async-start | bytes 32768 | tf_op jit(solution)/shard_map/all_to_all | solution.py:371
  10.2 0.0 copy-start.5
  10.2 3.7 %collective-permute-start.2 = (bf16[16,2176]{1,0:T(8,128)(2,1)}, bf16[16,2176]{1,0:T(8,128)(2,1)S(1)}, u32[]{:S(2)}, u32[]{:S(2)}) collective-permute-start(bf16[16,2176]{1,0:T(8,128)(2,1)} %get-tuple-element.15), channel_id=1, source_target_pairs={{0,24},{1,25},{2,26},{3,27},{4,28},{5,29},{6,30},{7,31},{8,16},{9,... | collective-permute-start | bytes 208904 | tf_op jit(solution)/shard_map/ppermute | solution.py:35
  13.9 0.0 collective-permute-start.1
  13.9 0.8 collective-permute-start
  14.7 2.7 %all-to-all-done.refs_4_ = f32[32,1,128]{2,1,0:T(1,128)S(1)} async-done(((f32[32,1,128]{2,1,0:T(1,128)}), f32[32,1,128]{2,1,0:T(1,128)S(1)}, u32[]{:S(2)}, u32[]{:S(2)}) %all-to-all-start) | async-done | bytes 16416 | tf_op jit(solution)/shard_map/all_to_all | solution.py:371
  17.4 0.6 copy-done.3
  18.0 6.4 %shard_map.120 = (bf16[3,4,32,2048]{3,2,1,0:T(8,128)(2,1)}, bf16[32,3,8,1024]{3,2,1,0:T(8,128)(2,1)}) custom-call(f32[3,4,32,2048]{3,2,1,0:T(8,128)} %refs_0_.1, f32[3,4,32,2048]{3,2,1,0:T(8,128)} %refs_1_.3, f32[3,4,32,2048]{3,2,1,0:T(8,128)} %refs_2_.1, bf16[3,4,32,2048]{3,2,1,0:T(8,128)(2,1)} %refs_3_.1, f32[32,1,128]{2,1,0:T(1,128)} %copy-done.3), custom_call_target="tpu_custom_call" | custom-call | tf_op jit(solution)/shard_map/pallas_call | solution.py:264
  24.4 0.1 collective-permute-start.6
  24.5 0.0 copy-done.5
  24.5 0.0 collective-permute-done
  24.5 0.0 collective-permute-done.1
  24.6 0.0 collective-permute-done.2
  24.6 0.0 copy-start.4
  24.6 0.7 collective-permute-start.5
  25.3 1.3 %collective-permute-start.4 = (bf16[64,2176]{1,0:T(8,128)(2,1)S(1)}, bf16[64,2176]{1,0:T(8,128)(2,1)S(1)}, u32[]{:S(2)}, u32[]{:S(2)}) collective-permute-start(bf16[64,2176]{1,0:T(8,128)(2,1)S(1)} %constant_dynamic-update-slice_fusion.refs_0_), channel_id=1, source_target_pairs={{0,4},{1,5},{2,6},{3,7},{4,0},{5,1},{6,2},{7,3},{8,12},{9,13},{10,... | collective-permute-start | bytes 835592 | tf_op jit(solution)/shard_map/ppermute | solution.py:35
  26.6 1.5 %collective-permute-start.3 = (bf16[64,2176]{1,0:T(8,128)(2,1)S(1)}, bf16[64,2176]{1,0:T(8,128)(2,1)S(1)}, u32[]{:S(2)}, u32[]{:S(2)}) collective-permute-start(bf16[64,2176]{1,0:T(8,128)(2,1)S(1)} %constant_dynamic-update-slice_fusion.refs_0_), channel_id=1, source_target_pairs={{0,2},{1,3},{2,0},{3,1},{4,6},{5,7},{6,4},{7,5},{8,10},{9,11},{10,... | collective-permute-start | bytes 835592 | tf_op jit(solution)/shard_map/ppermute | solution.py:35
  28.2 7.0 %collective-permute-done.5.refs_3_ = bf16[64,2176]{1,0:T(8,128)(2,1)S(1)} collective-permute-done((bf16[64,2176]{1,0:T(8,128)(2,1)S(1)}, bf16[64,2176]{1,0:T(8,128)(2,1)S(1)}, u32[]{:S(2)}, u32[]{:S(2)}) %collective-permute-start.5) | collective-permute-done | bytes 278560 | tf_op jit(solution)/shard_map/ppermute | solution.py:35
  35.1 4.9 %collective-permute-done.4.refs_2_ = bf16[64,2176]{1,0:T(8,128)(2,1)S(1)} collective-permute-done((bf16[64,2176]{1,0:T(8,128)(2,1)S(1)}, bf16[64,2176]{1,0:T(8,128)(2,1)S(1)}, u32[]{:S(2)}, u32[]{:S(2)}) %collective-permute-start.4) | collective-permute-done | bytes 278560 | tf_op jit(solution)/shard_map/ppermute | solution.py:35
  40.0 0.0 collective-permute-done.3.refs_1_
  40.1 0.0 collective-permute-done.6.refs_5_
  40.1 1.4 %copy-done = bf16[3,4,32,2048]{3,2,1,0:T(8,128)(2,1)S(1)} copy-done((bf16[3,4,32,2048]{3,2,1,0:T(8,128)(2,1)S(1)}, bf16[3,4,32,2048]{3,2,1,0:T(8,128)(2,1)}, u32[]{:S(2)}) %copy-start) | copy-done | bytes 1572888
  41.5 1.1 %shard_map.122 = (f32[64,2048]{1,0:T(8,128)S(1)}, bf16[64,2048]{1,0:T(8,128)(2,1)S(1)}, bf16[64,2048]{1,0:T(8,128)(2,1)S(1)}, bf16[64,2048]{1,0:T(8,128)(2,1)S(1)}) custom-call(bf16[64,2176]{1,0:T(8,128)(2,1)S(1)} %constant_dynamic-update-slice_fusion.refs_0_, bf16[64,2176]{1,0:T(8,128)(2,1)S(1)} %collective-permute-done.3.refs_1_, ...), custom_call_target="tpu_custom_call" | custom-call | tf_op jit(solution)/shard_map/pallas_call | solution.py:180
  42.6 1.2 %collective-permute-start.7 = (bf16[64,2048]{1,0:T(8,128)(2,1)S(1)}, bf16[64,2048]{1,0:T(8,128)(2,1)S(1)}, u32[]{:S(2)}, u32[]{:S(2)}) collective-permute-start(bf16[64,2048]{1,0:T(8,128)(2,1)S(1)} %get-tuple-element.18), channel_id=1, source_target_pairs={{0,6},{1,7},{2,4},{3,5},{4,2},{5,3},{6,0},{7,1},{8,14},{9,15},{10,... | collective-permute-start | bytes 786440 | tf_op jit(solution)/shard_map/ppermute | solution.py:35
  43.8 1.3 %collective-permute-start.8 = (bf16[64,2048]{1,0:T(8,128)(2,1)S(1)}, bf16[64,2048]{1,0:T(8,128)(2,1)S(1)}, u32[]{:S(2)}, u32[]{:S(2)}) collective-permute-start(bf16[64,2048]{1,0:T(8,128)(2,1)S(1)} %get-tuple-element.19), channel_id=1, source_target_pairs={{0,4},{1,5},{2,6},{3,7},{4,0},{5,1},{6,2},{7,3},{8,12},{9,13},{10,... | collective-permute-start | bytes 786440 | tf_op jit(solution)/shard_map/ppermute | solution.py:35
  45.2 1.0 %collective-permute-start.9 = (bf16[64,2048]{1,0:T(8,128)(2,1)S(1)}, bf16[64,2048]{1,0:T(8,128)(2,1)}, u32[]{:S(2)}, u32[]{:S(2)}) collective-permute-start(bf16[64,2048]{1,0:T(8,128)(2,1)S(1)} %get-tuple-element.20), channel_id=1, source_target_pairs={{0,2},{1,3},{2,0},{3,1},{4,6},{5,7},{6,4},{7,5},{8,10},{9,11},{10,... | collective-permute-start | bytes 786440 | tf_op jit(solution)/shard_map/ppermute | solution.py:35
  46.1 3.0 %all-to-all-start.1 = ((bf16[32,3,8,1024]{3,2,1,0:T(8,128)(2,1)}), bf16[32,3,8,1024]{3,2,1,0:T(8,128)(2,1)S(1)}, u32[]{:S(2)}, u32[]{:S(2)}) async-start(bf16[32,3,8,1024]{3,2,1,0:T(8,128)(2,1)} %get-tuple-element.14), calls=%async_computation.1 | async-start | bytes 3145728 | tf_op jit(solution)/shard_map/all_to_all | solution.py:395
  49.2 0.0 copy-done.4
  49.2 0.6 slice_reduce_fusion
  50.5 0.0 copy-start.1
  50.5 2.3 %collective-permute-done.7 = bf16[64,2048]{1,0:T(8,128)(2,1)S(1)} collective-permute-done((bf16[64,2048]{1,0:T(8,128)(2,1)S(1)}, bf16[64,2048]{1,0:T(8,128)(2,1)S(1)}, u32[]{:S(2)}, u32[]{:S(2)}) %collective-permute-start.7) | collective-permute-done | bytes 262176 | tf_op jit(solution)/shard_map/ppermute | solution.py:35
  52.8 8.0 %collective-permute-done.8 = bf16[64,2048]{1,0:T(8,128)(2,1)S(1)} collective-permute-done((bf16[64,2048]{1,0:T(8,128)(2,1)S(1)}, bf16[64,2048]{1,0:T(8,128)(2,1)S(1)}, u32[]{:S(2)}, u32[]{:S(2)}) %collective-permute-start.8) | collective-permute-done | bytes 262176 | tf_op jit(solution)/shard_map/ppermute | solution.py:35
  60.8 3.0 %collective-permute-done.9 = bf16[64,2048]{1,0:T(8,128)(2,1)} collective-permute-done((bf16[64,2048]{1,0:T(8,128)(2,1)S(1)}, bf16[64,2048]{1,0:T(8,128)(2,1)}, u32[]{:S(2)}, u32[]{:S(2)}) %collective-permute-start.9) | collective-permute-done | bytes 262176 | tf_op jit(solution)/shard_map/ppermute | solution.py:35
  63.8 1.1 %fusion.3 = (bf16[64,2048]{1,0:T(8,128)(2,1)S(1)}, f32[64,2048]{1,0:T(8,128)S(1)}) fusion(bf16[64,2048]{1,0:T(8,128)(2,1)} %collective-permute-done.9, bf16[64,2048]{1,0:T(8,128)(2,1)S(1)} %collective-permute-done.8, f32[64,2048]{1,0:T(8,128)S(1)} %get-tuple-element.17, bf16[64,2048]{1,0:T(8,128)(2,1)S(1)} %collective-permute-done.7), kind=kLoop, calls=%fused_computation.15 | loop fusion | flops 917504 | bytes 2097152 | tf_op jit(solution)/shard_map/convert.2
  64.9 0.1 collective-permute-start.10
  65.0 0.1 collective-permute-start.12
  65.1 0.0 copy-start.2
  65.1 4.3 %collective-permute-start.11 = (bf16[16,2048]{1,0:T(8,128)(2,1)S(1)}, bf16[16,2048]{1,0:T(8,128)(2,1)S(1)}, u32[]{:S(2)}, u32[]{:S(2)}) collective-permute-start(bf16[16,2048]{1,0:T(8,128)(2,1)S(1)} %get-tuple-element.28), channel_id=1, source_target_pairs={{0,16},{1,17},{2,18},{3,19},{4,20},{5,21},{6,22},{7,23},{8,24},{9,... | collective-permute-start | bytes 196616 | tf_op jit(solution)/shard_map/ppermute | solution.py:35
  69.4 0.0 copy-done.1
  69.4 7.3 %multiply_subtract_fusion = (f32[3,4,32,2048]{3,2,1,0:T(8,128)}, f32[3,4,32,2048]{3,2,1,0:T(8,128)}, f32[3,4,32,2048]{3,2,1,0:T(8,128)}) fusion(f32[3,4,32,2048]{3,2,1,0:T(8,128)} %refs_0_.1, f32[]{:T(128)S(6)} %min_shard_map.3, bf16[3,4,32,2048]{3,2,1,0:T(8,128)(2,1)S(1)} %copy-done.1, f32[3,4,32,2048]{3,2,1,0:T(8,128)} %refs_1_.3, f32[3,4,32,2048]{3,2,1,0:T(8,128)} %refs_2_.1), kind=kLoop, calls=%fused_computation.2 | loop fusion | flops 13369344 | bytes 20447236 | tf_op jit(solution)/shard_map/sub | solution.py:31
  76.7 4.5 %collective-permute-done.10 = bf16[16,2048]{1,0:T(8,128)(2,1)S(1)} collective-permute-done((bf16[16,2048]{1,0:T(8,128)(2,1)S(1)}, bf16[16,2048]{1,0:T(8,128)(2,1)S(1)}, u32[]{:S(2)}, u32[]{:S(2)}) %collective-permute-start.10) | collective-permute-done | bytes 65568 | tf_op jit(solution)/shard_map/ppermute | solution.py:35
  81.1 0.0 collective-permute-done.12
  81.1 11.2 %collective-permute-done.11 = bf16[16,2048]{1,0:T(8,128)(2,1)S(1)} collective-permute-done((bf16[16,2048]{1,0:T(8,128)(2,1)S(1)}, bf16[16,2048]{1,0:T(8,128)(2,1)S(1)}, u32[]{:S(2)}, u32[]{:S(2)}) %collective-permute-start.11) | collective-permute-done | bytes 65568 | tf_op jit(solution)/shard_map/ppermute | solution.py:35
  92.5 0.0 copy-done.2
  92.5 0.7 add_convert_fusion
  93.1 0.0 all-to-all-done.1.source
  93.1 1.4 %shard_map.121 = bf16[3,128,2048]{2,1,0:T(8,128)(2,1)} custom-call(bf16[32,3,8,1024]{3,2,1,0:T(8,128)(2,1)S(1)} %all-to-all-done.1.source), custom_call_target="tpu_custom_call" | custom-call | tf_op jit(solution)/shard_map/pallas_call | solution.py:334
  (9 shorter events, 0.1 us)
Async XLA Ops:
  2.9 14.5 %all-to-all-start = ((f32[32,1,128]{2,1,0:T(1,128)}), f32[32,1,128]{2,1,0:T(1,128)S(1)}, u32[]{:S(2)}, u32[]{:S(2)}) async-start(f32[32,1,128]{2,1,0:T(1,128)} %get-tuple-element.13), calls=%async_computation | async-start | bytes 32768 | tf_op jit(solution)/shard_map/all_to_all | solution.py:371
  10.2 14.3 %copy-start.5 = (bf16[16,2176]{1,0:T(8,128)(2,1)S(1)}, bf16[16,2176]{1,0:T(8,128)(2,1)}, u32[]{:S(2)}) copy-start(bf16[16,2176]{1,0:T(8,128)(2,1)} %get-tuple-element.15) | copy-start | bytes 208900
  10.2 14.3 %collective-permute-start.2 = (bf16[16,2176]{1,0:T(8,128)(2,1)}, bf16[16,2176]{1,0:T(8,128)(2,1)S(1)}, u32[]{:S(2)}, u32[]{:S(2)}) collective-permute-start(bf16[16,2176]{1,0:T(8,128)(2,1)} %get-tuple-element.15), channel_id=1, source_target_pairs={{0,24},{1,25},{2,26},{3,27},{4,28},{5,29},{6,30},{7,31},{8,16},{9,... | collective-permute-start | bytes 208904 | tf_op jit(solution)/shard_map/ppermute | solution.py:35
  13.9 10.6 %collective-permute-start.1 = (bf16[16,2176]{1,0:T(8,128)(2,1)}, bf16[16,2176]{1,0:T(8,128)(2,1)S(1)}, u32[]{:S(2)}, u32[]{:S(2)}) collective-permute-start(bf16[16,2176]{1,0:T(8,128)(2,1)} %get-tuple-element.15), channel_id=1, source_target_pairs={{0,16},{1,17},{2,18},{3,19},{4,20},{5,21},{6,22},{7,23},{8,24},{9,... | collective-permute-start | bytes 208904 | tf_op jit(solution)/shard_map/ppermute | solution.py:35
  13.9 10.6 %collective-permute-start = (bf16[16,2176]{1,0:T(8,128)(2,1)}, bf16[16,2176]{1,0:T(8,128)(2,1)S(1)}, u32[]{:S(2)}, u32[]{:S(2)}) collective-permute-start(bf16[16,2176]{1,0:T(8,128)(2,1)} %get-tuple-element.15), channel_id=1, source_target_pairs={{0,8},{1,9},{2,10},{3,11},{4,12},{5,13},{6,14},{7,15},{8,0},{9,1},... | collective-permute-start | bytes 208904 | tf_op jit(solution)/shard_map/ppermute | solution.py:35
  17.4 0.6 copy-start.3
  24.4 15.6 %collective-permute-start.6 = (bf16[3,4,32,2048]{3,2,1,0:T(8,128)(2,1)}, bf16[3,4,32,2048]{3,2,1,0:T(8,128)(2,1)S(1)}, u32[]{:S(2)}, u32[]{:S(2)}) collective-permute-start(bf16[3,4,32,2048]{3,2,1,0:T(8,128)(2,1)} %get-tuple-element.16.refs_4_), channel_id=1, source_target_pairs={{0,1},{1,0},{2,3},{3,2},{4,5},{5,4},{6,7},{7,6},{8,9},{9,8},{10,11... | collective-permute-start | bytes 4718600 | tf_op jit(solution)/shard_map/ppermute | solution.py:35
  24.6 24.6 %copy-start.4 = (f32[32,1,128]{2,1,0:T(1,128)S(1)}, f32[32,1,128]{2,1,0:T(1,128)}, u32[]{:S(2)}) copy-start(f32[32,1,128]{2,1,0:T(1,128)} %copy-done.3) | copy-start | bytes 49156
  24.6 10.5 %collective-permute-start.5 = (bf16[64,2176]{1,0:T(8,128)(2,1)S(1)}, bf16[64,2176]{1,0:T(8,128)(2,1)S(1)}, u32[]{:S(2)}, u32[]{:S(2)}) collective-permute-start(bf16[64,2176]{1,0:T(8,128)(2,1)S(1)} %constant_dynamic-update-slice_fusion.refs_0_), channel_id=1, source_target_pairs={{0,6},{1,7},{2,4},{3,5},{4,2},{5,3},{6,0},{7,1},{8,14},{9,15},{10,... | collective-permute-start | bytes 835592 | tf_op jit(solution)/shard_map/ppermute | solution.py:35
  25.3 14.7 %collective-permute-start.4 = (bf16[64,2176]{1,0:T(8,128)(2,1)S(1)}, bf16[64,2176]{1,0:T(8,128)(2,1)S(1)}, u32[]{:S(2)}, u32[]{:S(2)}) collective-permute-start(bf16[64,2176]{1,0:T(8,128)(2,1)S(1)} %constant_dynamic-update-slice_fusion.refs_0_), channel_id=1, source_target_pairs={{0,4},{1,5},{2,6},{3,7},{4,0},{5,1},{6,2},{7,3},{8,12},{9,13},{10,... | collective-permute-start | bytes 835592 | tf_op jit(solution)/shard_map/ppermute | solution.py:35
  26.6 13.4 %collective-permute-start.3 = (bf16[64,2176]{1,0:T(8,128)(2,1)S(1)}, bf16[64,2176]{1,0:T(8,128)(2,1)S(1)}, u32[]{:S(2)}, u32[]{:S(2)}) collective-permute-start(bf16[64,2176]{1,0:T(8,128)(2,1)S(1)} %constant_dynamic-update-slice_fusion.refs_0_), channel_id=1, source_target_pairs={{0,2},{1,3},{2,0},{3,1},{4,6},{5,7},{6,4},{7,5},{8,10},{9,11},{10,... | collective-permute-start | bytes 835592 | tf_op jit(solution)/shard_map/ppermute | solution.py:35
  40.1 1.4 %copy-start = (bf16[3,4,32,2048]{3,2,1,0:T(8,128)(2,1)S(1)}, bf16[3,4,32,2048]{3,2,1,0:T(8,128)(2,1)}, u32[]{:S(2)}) copy-start(bf16[3,4,32,2048]{3,2,1,0:T(8,128)(2,1)} %get-tuple-element.16.refs_4_) | copy-start | bytes 4718596
  42.6 10.2 %collective-permute-start.7 = (bf16[64,2048]{1,0:T(8,128)(2,1)S(1)}, bf16[64,2048]{1,0:T(8,128)(2,1)S(1)}, u32[]{:S(2)}, u32[]{:S(2)}) collective-permute-start(bf16[64,2048]{1,0:T(8,128)(2,1)S(1)} %get-tuple-element.18), channel_id=1, source_target_pairs={{0,6},{1,7},{2,4},{3,5},{4,2},{5,3},{6,0},{7,1},{8,14},{9,15},{10,... | collective-permute-start | bytes 786440 | tf_op jit(solution)/shard_map/ppermute | solution.py:35
  43.8 17.0 %collective-permute-start.8 = (bf16[64,2048]{1,0:T(8,128)(2,1)S(1)}, bf16[64,2048]{1,0:T(8,128)(2,1)S(1)}, u32[]{:S(2)}, u32[]{:S(2)}) collective-permute-start(bf16[64,2048]{1,0:T(8,128)(2,1)S(1)} %get-tuple-element.19), channel_id=1, source_target_pairs={{0,4},{1,5},{2,6},{3,7},{4,0},{5,1},{6,2},{7,3},{8,12},{9,13},{10,... | collective-permute-start | bytes 786440 | tf_op jit(solution)/shard_map/ppermute | solution.py:35
  45.2 18.6 %collective-permute-start.9 = (bf16[64,2048]{1,0:T(8,128)(2,1)S(1)}, bf16[64,2048]{1,0:T(8,128)(2,1)}, u32[]{:S(2)}, u32[]{:S(2)}) collective-permute-start(bf16[64,2048]{1,0:T(8,128)(2,1)S(1)} %get-tuple-element.20), channel_id=1, source_target_pairs={{0,2},{1,3},{2,0},{3,1},{4,6},{5,7},{6,4},{7,5},{8,10},{9,11},{10,... | collective-permute-start | bytes 786440 | tf_op jit(solution)/shard_map/ppermute | solution.py:35
  46.1 47.0 %all-to-all-start.1 = ((bf16[32,3,8,1024]{3,2,1,0:T(8,128)(2,1)}), bf16[32,3,8,1024]{3,2,1,0:T(8,128)(2,1)S(1)}, u32[]{:S(2)}, u32[]{:S(2)}) async-start(bf16[32,3,8,1024]{3,2,1,0:T(8,128)(2,1)} %get-tuple-element.14), calls=%async_computation.1 | async-start | bytes 3145728 | tf_op jit(solution)/shard_map/all_to_all | solution.py:395
  50.5 18.9 %copy-start.1 = (bf16[3,4,32,2048]{3,2,1,0:T(8,128)(2,1)S(1)}, bf16[3,4,32,2048]{3,2,1,0:T(8,128)(2,1)}, u32[]{:S(2)}) copy-start(bf16[3,4,32,2048]{3,2,1,0:T(8,128)(2,1)} %refs_3_.1) | copy-start | bytes 4718596
  64.9 16.2 %collective-permute-start.10 = (bf16[16,2048]{1,0:T(8,128)(2,1)S(1)}, bf16[16,2048]{1,0:T(8,128)(2,1)S(1)}, u32[]{:S(2)}, u32[]{:S(2)}) collective-permute-start(bf16[16,2048]{1,0:T(8,128)(2,1)S(1)} %get-tuple-element.26), channel_id=1, source_target_pairs={{0,24},{1,25},{2,26},{3,27},{4,28},{5,29},{6,30},{7,31},{8,16},{9,... | collective-permute-start | bytes 196616 | tf_op jit(solution)/shard_map/ppermute | solution.py:35
  65.0 16.2 %collective-permute-start.12 = (bf16[16,2048]{1,0:T(8,128)(2,1)S(1)}, bf16[16,2048]{1,0:T(8,128)(2,1)S(1)}, u32[]{:S(2)}, u32[]{:S(2)}) collective-permute-start(bf16[16,2048]{1,0:T(8,128)(2,1)S(1)} %get-tuple-element.27), channel_id=1, source_target_pairs={{0,8},{1,9},{2,10},{3,11},{4,12},{5,13},{6,14},{7,15},{8,0},{9,1},... | collective-permute-start | bytes 196616 | tf_op jit(solution)/shard_map/ppermute | solution.py:35
  65.1 27.4 %copy-start.2 = (bf16[4,4,2048]{2,1,0:T(4,128)(2,1)S(1)}, bf16[4,4,2048]{2,1,0:T(4,128)(2,1)}, u32[]{:S(2)}) copy-start(bf16[4,4,2048]{2,1,0:T(4,128)(2,1)} %refs_1_.2) | copy-start | bytes 196612
  65.1 27.3 %collective-permute-start.11 = (bf16[16,2048]{1,0:T(8,128)(2,1)S(1)}, bf16[16,2048]{1,0:T(8,128)(2,1)S(1)}, u32[]{:S(2)}, u32[]{:S(2)}) collective-permute-start(bf16[16,2048]{1,0:T(8,128)(2,1)S(1)} %get-tuple-element.28), channel_id=1, source_target_pairs={{0,16},{1,17},{2,18},{3,19},{4,20},{5,21},{6,22},{7,23},{8,24},{9,... | collective-permute-start | bytes 196616 | tf_op jit(solution)/shard_map/ppermute | solution.py:35

commit v2 on v1

--- a/solution.py
+++ b/solution.py
@@ -123,7 +123,7 @@
             jax.ShapeDtypeStruct((receivers, 1, lanes), jnp.float32),
             jax.ShapeDtypeStruct((steps * row_count, model_width + lanes), jnp.bfloat16),
         ),
-        limit=60,
+        limit=54,
         in_specs=[hbm] * 5,
         scratch_shapes=[pltpu.VMEM((chunks, extent, flat.shape[1]), flat.dtype)]
         + [pltpu.VMEM(array.shape, array.dtype) for array in arrays]
@@ -196,10 +196,8 @@
     second_scale = 1.0 / (1.0 - beta_two**step_count)
 
     def kernel(*refs):
-        sources, shared, rounded, ordered = refs[:4], refs[4], refs[5], refs[6]
-        buffers, packed, plain, totals, got, put, summed = refs[7:11], *refs[11:17]
-        fetch = pltpu.make_async_copy(shared, totals, summed.at[0])
-        fetch.start()
+        sources, totals, rounded, ordered = refs[:4], refs[4], refs[5], refs[6]
+        buffers, packed, plain, got, put = refs[7:11], *refs[11:15]
 
         def place(b):
             return lax.div(b, expert_count), lax.rem(b, expert_count)
@@ -226,7 +224,6 @@
             return carry
 
         lax.fori_loop(0, blocks, issue, 0)
-        fetch.wait()
         squares = jnp.sum(totals[:, :, :1])
         clip = jnp.minimum(1.0, lax.rsqrt(jnp.full((1, 1), squares) / entries + norm_eps))
         one_slope = clip * ((1.0 - beta_one) * first_scale)
@@ -269,17 +266,15 @@
                 (expert_count * strips, kinds, pack * strip_width, width), jnp.bfloat16
             ),
         ),
-        limit=60,
-        in_specs=[hbm] * 5,
+        limit=53,
+        in_specs=[hbm] * 4 + [vmem],
         out_specs=(hbm, hbm),
         scratch_shapes=[pltpu.VMEM((blocks,) + own, array.dtype) for array in inputs]
         + [
             pltpu.VMEM((blocks, strips, pack * strip_width, width), jnp.bfloat16),
             pltpu.VMEM((blocks,) + own, jnp.bfloat16),
-            pltpu.VMEM(sums.shape, sums.dtype),
             pltpu.SemaphoreType.DMA((4, blocks)),
             pltpu.SemaphoreType.DMA((2, blocks)),
-            pltpu.SemaphoreType.DMA((1,)),
         ],
     )(*inputs, sums)
 

time: 94.9 us -> 94.2 us (level)
    unnamed x15 -> x11, local copies, waits for them, and re-layouts: 2.07 us -> 1.46 us
where the time goes in v2:
time: 94.2 us; the launch traced here: 93.9 us
  waiting for transfers between devices  43.6 us (46%)
  starting transfers between devices  26.4 us (28%)
  Pallas kernels  11.2 us (12%)
  other arithmetic  9.7 us (10%)
  local copies, waits for them, and re-layouts  1.53 us (2%)
  between operations  1.51 us (2%)
    ppermute x13, waiting for transfers between devices, exchange(): lax.ppermute(value, 'dp', [(i, i ^ offset) for i in range(member_count)])  40.9 us
    ppermute x13, starting transfers between devices, exchange(): lax.ppermute(value, 'dp', [(i, i ^ offset) for i in range(member_count)])  16.1 us
    all_to_all x1, starting transfers between devices, per_device(): sums = lax.all_to_all(sums, 'dp', split_axis=0, concat_axis=0, tiled=True)  7.33 us
    sub x1, other arithmetic, adam_update(): master - learn_rate * (update + decay_rate * master)  7.3 us
    pallas_call x1, Pallas kernels, serve_step(): call(kernel, (jax.ShapeDtypeStruct((kinds,) + master.shape[1:], jnp.bfloa...  6.36 us
    all_to_all x1, starting transfers between devices, per_device(): lax.all_to_all(ordered, 'dp', split_axis=0, concat_axis=0, tiled=True)  3 us
    all_to_all x1, waiting for transfers between devices, per_device(): sums = lax.all_to_all(sums, 'dp', split_axis=0, concat_axis=0, tiled=True)  2.71 us
    pallas_call x1, Pallas kernels, prepare(): call(kernel, (jax.ShapeDtypeStruct((receivers, 1, lanes), jnp.float32), j...  2.25 us
  transfers between devices with their start and end apart: 15, of which 8 were waited for; matrix products, arithmetic and copies ran while one was open for 10% of the time, Pallas kernels for 7%

profile of v2, /device:TPU:0, one launch (start us, length us, event | category | flops | bytes accessed | tf_op | source)
XLA Modules:
  0.0 93.9 jit_solution(12599580919943902527)
XLA Ops:
  0.6 2.3 %shard_map.119 = (f32[32,1,128]{2,1,0:T(1,128)}, bf16[16,2176]{1,0:T(8,128)(2,1)}) custom-call(bf16[384,2048]{1,0:T(8,128)(2,1)} %bitcast.4, bf16[4,4,2048]{2,1,0:T(4,128)(2,1)} %refs_1_.2, f32[1,2048]{1,0:T(1,128)} %bitcast.5, s32[4,2,4]{2,1,0:T(2,128)} %bitcast.6, f32[4,2,4]{2,1,0:T(2,128)} %bitcast.7), custom_call_target="tpu_custom_call" | custom-call | tf_op jit(solution)/shard_map/pallas_call | solution.py:120
  2.9 7.3 %all-to-all-start = ((f32[32,1,128]{2,1,0:T(1,128)}), f32[32,1,128]{2,1,0:T(1,128)S(1)}, u32[]{:S(2)}, u32[]{:S(2)}) async-start(f32[32,1,128]{2,1,0:T(1,128)} %get-tuple-element.13), calls=%async_computation | async-start | bytes 32768 | tf_op jit(solution)/shard_map/all_to_all | solution.py:366
  10.2 0.0 copy-start.3
  10.2 3.7 %collective-permute-start.2 = (bf16[16,2176]{1,0:T(8,128)(2,1)}, bf16[16,2176]{1,0:T(8,128)(2,1)S(1)}, u32[]{:S(2)}, u32[]{:S(2)}) collective-permute-start(bf16[16,2176]{1,0:T(8,128)(2,1)} %get-tuple-element.15), channel_id=1, source_target_pairs={{0,24},{1,25},{2,26},{3,27},{4,28},{5,29},{6,30},{7,31},{8,16},{9,... | collective-permute-start | bytes 208904 | tf_op jit(solution)/shard_map/ppermute | solution.py:35
  13.9 0.0 collective-permute-start.1
  13.9 0.8 collective-permute-start
  14.7 2.7 %all-to-all-done.refs_4_ = f32[32,1,128]{2,1,0:T(1,128)S(1)} async-done(((f32[32,1,128]{2,1,0:T(1,128)}), f32[32,1,128]{2,1,0:T(1,128)S(1)}, u32[]{:S(2)}, u32[]{:S(2)}) %all-to-all-start) | async-done | bytes 16416 | tf_op jit(solution)/shard_map/all_to_all | solution.py:366
  17.4 6.4 %shard_map.120 = (bf16[3,4,32,2048]{3,2,1,0:T(8,128)(2,1)}, bf16[32,3,8,1024]{3,2,1,0:T(8,128)(2,1)}) custom-call(f32[3,4,32,2048]{3,2,1,0:T(8,128)} %refs_0_.1, f32[3,4,32,2048]{3,2,1,0:T(8,128)} %refs_1_.3, f32[3,4,32,2048]{3,2,1,0:T(8,128)} %refs_2_.1, bf16[3,4,32,2048]{3,2,1,0:T(8,128)(2,1)} %refs_3_.1, f32[32,1,128]{2,1,0:T(1,128)S(1)} %all-to-all-done.refs_4_), custom_call_target="tpu_custom_call" | custom-call | tf_op jit(solution)/shard_map/pallas_call | solution.py:261
  23.8 0.1 collective-permute-start.6
  23.9 0.0 copy-done.3
  23.9 0.0 collective-permute-done
  23.9 0.0 collective-permute-done.1
  23.9 0.0 collective-permute-done.2
  24.0 0.7 collective-permute-start.5
  24.7 1.3 %collective-permute-start.4 = (bf16[64,2176]{1,0:T(8,128)(2,1)S(1)}, bf16[64,2176]{1,0:T(8,128)(2,1)S(1)}, u32[]{:S(2)}, u32[]{:S(2)}) collective-permute-start(bf16[64,2176]{1,0:T(8,128)(2,1)S(1)} %constant_dynamic-update-slice_fusion.refs_0_), channel_id=1, source_target_pairs={{0,4},{1,5},{2,6},{3,7},{4,0},{5,1},{6,2},{7,3},{8,12},{9,13},{10,... | collective-permute-start | bytes 835592 | tf_op jit(solution)/shard_map/ppermute | solution.py:35
  26.0 1.5 %collective-permute-start.3 = (bf16[64,2176]{1,0:T(8,128)(2,1)S(1)}, bf16[64,2176]{1,0:T(8,128)(2,1)S(1)}, u32[]{:S(2)}, u32[]{:S(2)}) collective-permute-start(bf16[64,2176]{1,0:T(8,128)(2,1)S(1)} %constant_dynamic-update-slice_fusion.refs_0_), channel_id=1, source_target_pairs={{0,2},{1,3},{2,0},{3,1},{4,6},{5,7},{6,4},{7,5},{8,10},{9,11},{10,... | collective-permute-start | bytes 835592 | tf_op jit(solution)/shard_map/ppermute | solution.py:35
  27.5 7.0 %collective-permute-done.5.refs_3_ = bf16[64,2176]{1,0:T(8,128)(2,1)S(1)} collective-permute-done((bf16[64,2176]{1,0:T(8,128)(2,1)S(1)}, bf16[64,2176]{1,0:T(8,128)(2,1)S(1)}, u32[]{:S(2)}, u32[]{:S(2)}) %collective-permute-start.5) | collective-permute-done | bytes 278560 | tf_op jit(solution)/shard_map/ppermute | solution.py:35
  34.5 4.9 %collective-permute-done.4.refs_2_ = bf16[64,2176]{1,0:T(8,128)(2,1)S(1)} collective-permute-done((bf16[64,2176]{1,0:T(8,128)(2,1)S(1)}, bf16[64,2176]{1,0:T(8,128)(2,1)S(1)}, u32[]{:S(2)}, u32[]{:S(2)}) %collective-permute-start.4) | collective-permute-done | bytes 278560 | tf_op jit(solution)/shard_map/ppermute | solution.py:35
  39.4 0.0 collective-permute-done.3.refs_1_
  39.4 0.0 collective-permute-done.6.refs_5_
  39.4 0.0 copy-start
  39.4 1.4 %copy-done = bf16[3,4,32,2048]{3,2,1,0:T(8,128)(2,1)S(1)} copy-done((bf16[3,4,32,2048]{3,2,1,0:T(8,128)(2,1)S(1)}, bf16[3,4,32,2048]{3,2,1,0:T(8,128)(2,1)}, u32[]{:S(2)}) %copy-start) | copy-done | bytes 1572888
  40.8 1.1 %shard_map.122 = (f32[64,2048]{1,0:T(8,128)S(1)}, bf16[64,2048]{1,0:T(8,128)(2,1)S(1)}, bf16[64,2048]{1,0:T(8,128)(2,1)S(1)}, bf16[64,2048]{1,0:T(8,128)(2,1)S(1)}) custom-call(bf16[64,2176]{1,0:T(8,128)(2,1)S(1)} %constant_dynamic-update-slice_fusion.refs_0_, bf16[64,2176]{1,0:T(8,128)(2,1)S(1)} %collective-permute-done.3.refs_1_, ...), custom_call_target="tpu_custom_call" | custom-call | tf_op jit(solution)/shard_map/pallas_call | solution.py:180
  42.0 1.2 %collective-permute-start.7 = (bf16[64,2048]{1,0:T(8,128)(2,1)S(1)}, bf16[64,2048]{1,0:T(8,128)(2,1)S(1)}, u32[]{:S(2)}, u32[]{:S(2)}) collective-permute-start(bf16[64,2048]{1,0:T(8,128)(2,1)S(1)} %get-tuple-element.18), channel_id=1, source_target_pairs={{0,6},{1,7},{2,4},{3,5},{4,2},{5,3},{6,0},{7,1},{8,14},{9,15},{10,... | collective-permute-start | bytes 786440 | tf_op jit(solution)/shard_map/ppermute | solution.py:35
  43.2 1.3 %collective-permute-start.8 = (bf16[64,2048]{1,0:T(8,128)(2,1)S(1)}, bf16[64,2048]{1,0:T(8,128)(2,1)S(1)}, u32[]{:S(2)}, u32[]{:S(2)}) collective-permute-start(bf16[64,2048]{1,0:T(8,128)(2,1)S(1)} %get-tuple-element.19), channel_id=1, source_target_pairs={{0,4},{1,5},{2,6},{3,7},{4,0},{5,1},{6,2},{7,3},{8,12},{9,13},{10,... | collective-permute-start | bytes 786440 | tf_op jit(solution)/shard_map/ppermute | solution.py:35
  44.5 1.0 %collective-permute-start.9 = (bf16[64,2048]{1,0:T(8,128)(2,1)S(1)}, bf16[64,2048]{1,0:T(8,128)(2,1)}, u32[]{:S(2)}, u32[]{:S(2)}) collective-permute-start(bf16[64,2048]{1,0:T(8,128)(2,1)S(1)} %get-tuple-element.20), channel_id=1, source_target_pairs={{0,2},{1,3},{2,0},{3,1},{4,6},{5,7},{6,4},{7,5},{8,10},{9,11},{10,... | collective-permute-start | bytes 786440 | tf_op jit(solution)/shard_map/ppermute | solution.py:35
  45.5 3.0 %all-to-all-start.1 = ((bf16[32,3,8,1024]{3,2,1,0:T(8,128)(2,1)}), bf16[32,3,8,1024]{3,2,1,0:T(8,128)(2,1)S(1)}, u32[]{:S(2)}, u32[]{:S(2)}) async-start(bf16[32,3,8,1024]{3,2,1,0:T(8,128)(2,1)} %get-tuple-element.14), calls=%async_computation.1 | async-start | bytes 3145728 | tf_op jit(solution)/shard_map/all_to_all | solution.py:390
  48.5 0.6 slice_reduce_fusion
  49.8 0.0 copy-start.1
  49.9 2.3 %collective-permute-done.7 = bf16[64,2048]{1,0:T(8,128)(2,1)S(1)} collective-permute-done((bf16[64,2048]{1,0:T(8,128)(2,1)S(1)}, bf16[64,2048]{1,0:T(8,128)(2,1)S(1)}, u32[]{:S(2)}, u32[]{:S(2)}) %collective-permute-start.7) | collective-permute-done | bytes 262176 | tf_op jit(solution)/shard_map/ppermute | solution.py:35
  52.1 8.0 %collective-permute-done.8 = bf16[64,2048]{1,0:T(8,128)(2,1)S(1)} collective-permute-done((bf16[64,2048]{1,0:T(8,128)(2,1)S(1)}, bf16[64,2048]{1,0:T(8,128)(2,1)S(1)}, u32[]{:S(2)}, u32[]{:S(2)}) %collective-permute-start.8) | collective-permute-done | bytes 262176 | tf_op jit(solution)/shard_map/ppermute | solution.py:35
  60.2 3.0 %collective-permute-done.9 = bf16[64,2048]{1,0:T(8,128)(2,1)} collective-permute-done((bf16[64,2048]{1,0:T(8,128)(2,1)S(1)}, bf16[64,2048]{1,0:T(8,128)(2,1)}, u32[]{:S(2)}, u32[]{:S(2)}) %collective-permute-start.9) | collective-permute-done | bytes 262176 | tf_op jit(solution)/shard_map/ppermute | solution.py:35
  63.2 1.1 %fusion.3 = (bf16[64,2048]{1,0:T(8,128)(2,1)S(1)}, f32[64,2048]{1,0:T(8,128)S(1)}) fusion(bf16[64,2048]{1,0:T(8,128)(2,1)} %collective-permute-done.9, bf16[64,2048]{1,0:T(8,128)(2,1)S(1)} %collective-permute-done.8, f32[64,2048]{1,0:T(8,128)S(1)} %get-tuple-element.17, bf16[64,2048]{1,0:T(8,128)(2,1)S(1)} %collective-permute-done.7), kind=kLoop, calls=%fused_computation.15 | loop fusion | flops 917504 | bytes 2097152 | tf_op jit(solution)/shard_map/convert.2
  64.3 0.1 collective-permute-start.10
  64.3 0.1 collective-permute-start.12
  64.4 0.0 copy-start.2
  64.4 4.3 %collective-permute-start.11 = (bf16[16,2048]{1,0:T(8,128)(2,1)S(1)}, bf16[16,2048]{1,0:T(8,128)(2,1)S(1)}, u32[]{:S(2)}, u32[]{:S(2)}) collective-permute-start(bf16[16,2048]{1,0:T(8,128)(2,1)S(1)} %get-tuple-element.28), channel_id=1, source_target_pairs={{0,16},{1,17},{2,18},{3,19},{4,20},{5,21},{6,22},{7,23},{8,24},{9,... | collective-permute-start | bytes 196616 | tf_op jit(solution)/shard_map/ppermute | solution.py:35
  68.7 0.0 copy-done.1
  68.7 7.3 %multiply_subtract_fusion = (f32[3,4,32,2048]{3,2,1,0:T(8,128)}, f32[3,4,32,2048]{3,2,1,0:T(8,128)}, f32[3,4,32,2048]{3,2,1,0:T(8,128)}) fusion(f32[3,4,32,2048]{3,2,1,0:T(8,128)} %refs_0_.1, f32[]{:T(128)S(6)} %min_shard_map.3, bf16[3,4,32,2048]{3,2,1,0:T(8,128)(2,1)S(1)} %copy-done.1, f32[3,4,32,2048]{3,2,1,0:T(8,128)} %refs_1_.3, f32[3,4,32,2048]{3,2,1,0:T(8,128)} %refs_2_.1), kind=kLoop, calls=%fused_computation.2 | loop fusion | flops 13369344 | bytes 20447236 | tf_op jit(solution)/shard_map/sub | solution.py:31
  76.0 4.5 %collective-permute-done.10 = bf16[16,2048]{1,0:T(8,128)(2,1)S(1)} collective-permute-done((bf16[16,2048]{1,0:T(8,128)(2,1)S(1)}, bf16[16,2048]{1,0:T(8,128)(2,1)S(1)}, u32[]{:S(2)}, u32[]{:S(2)}) %collective-permute-start.10) | collective-permute-done | bytes 65568 | tf_op jit(solution)/shard_map/ppermute | solution.py:35
  80.5 0.0 collective-permute-done.12
  80.5 11.2 %collective-permute-done.11 = bf16[16,2048]{1,0:T(8,128)(2,1)S(1)} collective-permute-done((bf16[16,2048]{1,0:T(8,128)(2,1)S(1)}, bf16[16,2048]{1,0:T(8,128)(2,1)S(1)}, u32[]{:S(2)}, u32[]{:S(2)}) %collective-permute-start.11) | collective-permute-done | bytes 65568 | tf_op jit(solution)/shard_map/ppermute | solution.py:35
  91.8 0.0 copy-done.2
  91.8 0.7 add_convert_fusion
  92.5 0.0 all-to-all-done.1.source
  92.5 1.4 %shard_map.121 = bf16[3,128,2048]{2,1,0:T(8,128)(2,1)} custom-call(bf16[32,3,8,1024]{3,2,1,0:T(8,128)(2,1)S(1)} %all-to-all-done.1.source), custom_call_target="tpu_custom_call" | custom-call | tf_op jit(solution)/shard_map/pallas_call | solution.py:329
  (7 shorter events, 0.1 us)
Async XLA Ops:
  2.9 14.5 %all-to-all-start = ((f32[32,1,128]{2,1,0:T(1,128)}), f32[32,1,128]{2,1,0:T(1,128)S(1)}, u32[]{:S(2)}, u32[]{:S(2)}) async-start(f32[32,1,128]{2,1,0:T(1,128)} %get-tuple-element.13), calls=%async_computation | async-start | bytes 32768 | tf_op jit(solution)/shard_map/all_to_all | solution.py:366
  10.2 13.6 %copy-start.3 = (bf16[16,2176]{1,0:T(8,128)(2,1)S(1)}, bf16[16,2176]{1,0:T(8,128)(2,1)}, u32[]{:S(2)}) copy-start(bf16[16,2176]{1,0:T(8,128)(2,1)} %get-tuple-element.15) | copy-start | bytes 208900
  10.2 13.7 %collective-permute-start.2 = (bf16[16,2176]{1,0:T(8,128)(2,1)}, bf16[16,2176]{1,0:T(8,128)(2,1)S(1)}, u32[]{:S(2)}, u32[]{:S(2)}) collective-permute-start(bf16[16,2176]{1,0:T(8,128)(2,1)} %get-tuple-element.15), channel_id=1, source_target_pairs={{0,24},{1,25},{2,26},{3,27},{4,28},{5,29},{6,30},{7,31},{8,16},{9,... | collective-permute-start | bytes 208904 | tf_op jit(solution)/shard_map/ppermute | solution.py:35
  13.9 10.0 %collective-permute-start.1 = (bf16[16,2176]{1,0:T(8,128)(2,1)}, bf16[16,2176]{1,0:T(8,128)(2,1)S(1)}, u32[]{:S(2)}, u32[]{:S(2)}) collective-permute-start(bf16[16,2176]{1,0:T(8,128)(2,1)} %get-tuple-element.15), channel_id=1, source_target_pairs={{0,16},{1,17},{2,18},{3,19},{4,20},{5,21},{6,22},{7,23},{8,24},{9,... | collective-permute-start | bytes 208904 | tf_op jit(solution)/shard_map/ppermute | solution.py:35
  13.9 10.0 %collective-permute-start = (bf16[16,2176]{1,0:T(8,128)(2,1)}, bf16[16,2176]{1,0:T(8,128)(2,1)S(1)}, u32[]{:S(2)}, u32[]{:S(2)}) collective-permute-start(bf16[16,2176]{1,0:T(8,128)(2,1)} %get-tuple-element.15), channel_id=1, source_target_pairs={{0,8},{1,9},{2,10},{3,11},{4,12},{5,13},{6,14},{7,15},{8,0},{9,1},... | collective-permute-start | bytes 208904 | tf_op jit(solution)/shard_map/ppermute | solution.py:35
  23.8 15.6 %collective-permute-start.6 = (bf16[3,4,32,2048]{3,2,1,0:T(8,128)(2,1)}, bf16[3,4,32,2048]{3,2,1,0:T(8,128)(2,1)S(1)}, u32[]{:S(2)}, u32[]{:S(2)}) collective-permute-start(bf16[3,4,32,2048]{3,2,1,0:T(8,128)(2,1)} %get-tuple-element.16.refs_4_), channel_id=1, source_target_pairs={{0,1},{1,0},{2,3},{3,2},{4,5},{5,4},{6,7},{7,6},{8,9},{9,8},{10,11... | collective-permute-start | bytes 4718600 | tf_op jit(solution)/shard_map/ppermute | solution.py:35
  24.0 10.5 %collective-permute-start.5 = (bf16[64,2176]{1,0:T(8,128)(2,1)S(1)}, bf16[64,2176]{1,0:T(8,128)(2,1)S(1)}, u32[]{:S(2)}, u32[]{:S(2)}) collective-permute-start(bf16[64,2176]{1,0:T(8,128)(2,1)S(1)} %constant_dynamic-update-slice_fusion.refs_0_), channel_id=1, source_target_pairs={{0,6},{1,7},{2,4},{3,5},{4,2},{5,3},{6,0},{7,1},{8,14},{9,15},{10,... | collective-permute-start | bytes 835592 | tf_op jit(solution)/shard_map/ppermute | solution.py:35
  24.7 14.7 %collective-permute-start.4 = (bf16[64,2176]{1,0:T(8,128)(2,1)S(1)}, bf16[64,2176]{1,0:T(8,128)(2,1)S(1)}, u32[]{:S(2)}, u32[]{:S(2)}) collective-permute-start(bf16[64,2176]{1,0:T(8,128)(2,1)S(1)} %constant_dynamic-update-slice_fusion.refs_0_), channel_id=1, source_target_pairs={{0,4},{1,5},{2,6},{3,7},{4,0},{5,1},{6,2},{7,3},{8,12},{9,13},{10,... | collective-permute-start | bytes 835592 | tf_op jit(solution)/shard_map/ppermute | solution.py:35
  26.0 13.4 %collective-permute-start.3 = (bf16[64,2176]{1,0:T(8,128)(2,1)S(1)}, bf16[64,2176]{1,0:T(8,128)(2,1)S(1)}, u32[]{:S(2)}, u32[]{:S(2)}) collective-permute-start(bf16[64,2176]{1,0:T(8,128)(2,1)S(1)} %constant_dynamic-update-slice_fusion.refs_0_), channel_id=1, source_target_pairs={{0,2},{1,3},{2,0},{3,1},{4,6},{5,7},{6,4},{7,5},{8,10},{9,11},{10,... | collective-permute-start | bytes 835592 | tf_op jit(solution)/shard_map/ppermute | solution.py:35
  39.4 1.4 %copy-start = (bf16[3,4,32,2048]{3,2,1,0:T(8,128)(2,1)S(1)}, bf16[3,4,32,2048]{3,2,1,0:T(8,128)(2,1)}, u32[]{:S(2)}) copy-start(bf16[3,4,32,2048]{3,2,1,0:T(8,128)(2,1)} %get-tuple-element.16.refs_4_) | copy-start | bytes 4718596
  42.0 10.2 %collective-permute-start.7 = (bf16[64,2048]{1,0:T(8,128)(2,1)S(1)}, bf16[64,2048]{1,0:T(8,128)(2,1)S(1)}, u32[]{:S(2)}, u32[]{:S(2)}) collective-permute-start(bf16[64,2048]{1,0:T(8,128)(2,1)S(1)} %get-tuple-element.18), channel_id=1, source_target_pairs={{0,6},{1,7},{2,4},{3,5},{4,2},{5,3},{6,0},{7,1},{8,14},{9,15},{10,... | collective-permute-start | bytes 786440 | tf_op jit(solution)/shard_map/ppermute | solution.py:35
  43.2 17.0 %collective-permute-start.8 = (bf16[64,2048]{1,0:T(8,128)(2,1)S(1)}, bf16[64,2048]{1,0:T(8,128)(2,1)S(1)}, u32[]{:S(2)}, u32[]{:S(2)}) collective-permute-start(bf16[64,2048]{1,0:T(8,128)(2,1)S(1)} %get-tuple-element.19), channel_id=1, source_target_pairs={{0,4},{1,5},{2,6},{3,7},{4,0},{5,1},{6,2},{7,3},{8,12},{9,13},{10,... | collective-permute-start | bytes 786440 | tf_op jit(solution)/shard_map/ppermute | solution.py:35
  44.5 18.6 %collective-permute-start.9 = (bf16[64,2048]{1,0:T(8,128)(2,1)S(1)}, bf16[64,2048]{1,0:T(8,128)(2,1)}, u32[]{:S(2)}, u32[]{:S(2)}) collective-permute-start(bf16[64,2048]{1,0:T(8,128)(2,1)S(1)} %get-tuple-element.20), channel_id=1, source_target_pairs={{0,2},{1,3},{2,0},{3,1},{4,6},{5,7},{6,4},{7,5},{8,10},{9,11},{10,... | collective-permute-start | bytes 786440 | tf_op jit(solution)/shard_map/ppermute | solution.py:35
  45.5 47.0 %all-to-all-start.1 = ((bf16[32,3,8,1024]{3,2,1,0:T(8,128)(2,1)}), bf16[32,3,8,1024]{3,2,1,0:T(8,128)(2,1)S(1)}, u32[]{:S(2)}, u32[]{:S(2)}) async-start(bf16[32,3,8,1024]{3,2,1,0:T(8,128)(2,1)} %get-tuple-element.14), calls=%async_computation.1 | async-start | bytes 3145728 | tf_op jit(solution)/shard_map/all_to_all | solution.py:390
  49.8 18.9 %copy-start.1 = (bf16[3,4,32,2048]{3,2,1,0:T(8,128)(2,1)S(1)}, bf16[3,4,32,2048]{3,2,1,0:T(8,128)(2,1)}, u32[]{:S(2)}) copy-start(bf16[3,4,32,2048]{3,2,1,0:T(8,128)(2,1)} %refs_3_.1) | copy-start | bytes 4718596
  64.3 16.2 %collective-permute-start.10 = (bf16[16,2048]{1,0:T(8,128)(2,1)S(1)}, bf16[16,2048]{1,0:T(8,128)(2,1)S(1)}, u32[]{:S(2)}, u32[]{:S(2)}) collective-permute-start(bf16[16,2048]{1,0:T(8,128)(2,1)S(1)} %get-tuple-element.26), channel_id=1, source_target_pairs={{0,24},{1,25},{2,26},{3,27},{4,28},{5,29},{6,30},{7,31},{8,16},{9,... | collective-permute-start | bytes 196616 | tf_op jit(solution)/shard_map/ppermute | solution.py:35
  64.3 16.2 %collective-permute-start.12 = (bf16[16,2048]{1,0:T(8,128)(2,1)S(1)}, bf16[16,2048]{1,0:T(8,128)(2,1)S(1)}, u32[]{:S(2)}, u32[]{:S(2)}) collective-permute-start(bf16[16,2048]{1,0:T(8,128)(2,1)S(1)} %get-tuple-element.27), channel_id=1, source_target_pairs={{0,8},{1,9},{2,10},{3,11},{4,12},{5,13},{6,14},{7,15},{8,0},{9,1},... | collective-permute-start | bytes 196616 | tf_op jit(solution)/shard_map/ppermute | solution.py:35
  64.4 27.4 %copy-start.2 = (bf16[4,4,2048]{2,1,0:T(4,128)(2,1)S(1)}, bf16[4,4,2048]{2,1,0:T(4,128)(2,1)}, u32[]{:S(2)}) copy-start(bf16[4,4,2048]{2,1,0:T(4,128)(2,1)} %refs_1_.2) | copy-start | bytes 196612
  64.4 27.3 %collective-permute-start.11 = (bf16[16,2048]{1,0:T(8,128)(2,1)S(1)}, bf16[16,2048]{1,0:T(8,128)(2,1)S(1)}, u32[]{:S(2)}, u32[]{:S(2)}) collective-permute-start(bf16[16,2048]{1,0:T(8,128)(2,1)S(1)} %get-tuple-element.28), channel_id=1, source_target_pairs={{0,16},{1,17},{2,18},{3,19},{4,20},{5,21},{6,22},{7,23},{8,24},{9,... | collective-permute-start | bytes 196616 | tf_op jit(solution)/shard_map/ppermute | solution.py:35
